TPU v7x, 256 devices: a whole 4x4x8 slice. The times are simulated.
256 devices in a mesh: temp: 64 (over y, z, core), mp: 4 (over x).
Axes of the slice: x: 4, y: 4, z: 8, core: 2. Of those that a mesh axis runs over, the one named last changes fastest.
Arguments:
- chains: bfloat16 [16384, 4096], P('temp', 'mp'), may hold values from 0 to 1
- weights: bfloat16 [4096, 4096], P('temp', 'mp'), may hold values from -0.375 to 0.375
- visible_bias: float32 [4096], replicated, may hold values from -6 to 6
- hidden_bias: float32 [4096], P('mp'), may hold values from -6 to 6
- inv_temps: float32 [64], P('temp'), may hold values from 0.25 to 1
- hidden_thresholds: int32 [2, 16384, 4096], P(None, 'temp', 'mp'), may hold values from 0 to 255
- visible_thresholds: int32 [2, 16384, 4096], P(None, 'temp'), may hold values from 0 to 255
- swap_phase: int32 [256], replicated, may hold values from 0 to 1
- swap_accept: int32 [16384], P('temp'), may hold values 0 or 1
Outputs:
- visible_out: bfloat16 [16384, 4096], P('temp', 'mp')
- hidden_out: bfloat16 [16384, 4096], P('temp', 'mp')
- energy: float32 [16384], P('temp')
Inputs may be any that keep to these rules, and one draw needn't show every extreme that they name: `swap_accept`: only entries r * 256 + c with r a lower partner of chain index c are read.
All inputs are finite; a program needn't handle non-finite values. No bound on the sum of `swap_accept` on one device may be relied on, other than what follows from the above.
Results may differ from a plain program's by a relative error of at most 0.0055.
Values may be sent and summed in bfloat16 or wider, within the bound.
A program may use at most 128 MiB of HBM per device.

v0:
```python
import jax
import jax.numpy as jnp
from jax import lax
from jax.sharding import PartitionSpec as P

NH = 4096
SWEEPS = 2


def copy_for_each(x, axis):
    copies = jnp.broadcast_to(x, (lax.axis_size(axis), *x.shape))
    return lax.all_to_all(copies, axis, split_axis=0, concat_axis=0, tiled=True)


def in_order(pieces, dim):
    pieces = jnp.moveaxis(pieces, 0, dim)
    shape = pieces.shape
    return pieces.reshape(*shape[:dim], shape[dim] * shape[dim + 1], *shape[dim + 2 :])


def gathered_copies(x, axis, dim):
    pieces = copy_for_each(x, axis)
    return in_order(pieces, dim)


def cut_along(x, dim, size):
    before, after = (x.shape[:dim], x.shape[dim + 1 :])
    return jnp.moveaxis(x.reshape(*before, size, -1, *after), dim, 0)


def sent_and_summed(x, axis, dim):
    pieces = cut_along(x, dim, lax.axis_size(axis))
    arrived = lax.all_to_all(pieces, axis, split_axis=0, concat_axis=0, tiled=True)
    return arrived.astype(jnp.float32).sum(axis=0)


def from_behind(value, axis, steps):
    count = lax.axis_size(axis)
    first, last = (max(0, -steps), min(count, count - steps))
    return lax.ppermute(value, axis, [(source, source + steps) for source in range(first, last)])


def logistic(thresholds):
    level = (thresholds.astype(jnp.float32) + 0.5) / 256.0
    return jnp.log(level) - jnp.log1p(-level)


def spread(visible_part):
    return gathered_copies(visible_part, "mp", 1)


def on_device(
    chains,
    weights,
    visible_bias,
    hidden_bias,
    inv_temps,
    hidden_thresholds,
    visible_thresholds,
    swap_phase,
    swap_accept,
):
    beta_dev = inv_temps[0]
    vis_width = chains.shape[1]
    offset = lax.axis_index("mp") * vis_width
    vis_bias_part = lax.dynamic_slice_in_dim(visible_bias, offset, vis_width, 0)
    visible_part = chains
    visible_full = spread(visible_part)
    weight_cols = lax.all_gather(weights, "temp", axis=0, tiled=True)
    hidden = None
    for sweep in range(SWEEPS):
        hidden_pre = jnp.dot(visible_full, weight_cols, preferred_element_type=jnp.float32)
        hidden = jax.nn.sigmoid(
            beta_dev * (hidden_pre + hidden_bias) + logistic(hidden_thresholds[sweep])
        ).astype(jnp.bfloat16)
        term = lax.dot_general(
            hidden, weight_cols, (((1,), (1,)), ((), ())), preferred_element_type=jnp.float32
        )
        visible_pre = sent_and_summed(term.astype(jnp.bfloat16), "mp", 1)
        vis_thr = lax.dynamic_slice_in_dim(visible_thresholds[sweep], offset, vis_width, 1)
        visible_part = jax.nn.sigmoid(
            beta_dev * (visible_pre + vis_bias_part) + logistic(vis_thr)
        ).astype(jnp.bfloat16)
        if sweep + 1 < SWEEPS:
            visible_full = spread(visible_part)
    replica = lax.axis_index("temp")
    total = lax.axis_size("temp")
    is_lower = (replica % 2 == swap_phase) & (replica + 1 < total)
    is_upper = ((replica - 1) % 2 == swap_phase) & (replica >= 1)
    decision = swap_accept.astype(jnp.bfloat16)
    low_vis, low_hid, low_dec = from_behind((visible_part, hidden, decision), "temp", 1)
    up_vis, up_hid = from_behind((visible_part, hidden), "temp", -1)
    take_up = (is_lower & (swap_accept == 1))[:, None]
    take_low = (is_upper & (low_dec > 0.5))[:, None]
    vis_out = jnp.where(take_up, up_vis, jnp.where(take_low, low_vis, visible_part))
    hid_out = jnp.where(take_up, up_hid, jnp.where(take_low, low_hid, hidden))
    vis_gathered = spread(vis_out)
    final_pre = jnp.dot(vis_gathered, weight_cols, preferred_element_type=jnp.float32) + hidden_bias
    soft_sum = jnp.sum(jax.nn.softplus(beta_dev * final_pre), axis=1)
    bias_sum = jnp.sum(vis_out.astype(jnp.float32) * vis_bias_part, axis=1)
    local_energy = -(beta_dev * bias_sum + soft_sum) / NH
    energy = lax.psum(local_energy, "mp")
    return (vis_out, hid_out, energy)


def solution(mesh):
    return jax.shard_map(
        on_device,
        mesh=mesh,
        in_specs=(
            P("temp", "mp"),
            P("temp", "mp"),
            P(),
            P("mp"),
            P("temp"),
            P(None, "temp", "mp"),
            P(None, "temp", None),
            P(),
            P("temp"),
        ),
        out_specs=(P("temp", "mp"), P("temp", "mp"), P("temp")),
        check_vma=False,
    )
```

profile of v0, /device:TPU:8, one launch (start us, length us, event | category | flops | bytes accessed | tf_op | source)
XLA Modules:
  0.0 281.8 jit_solution(7487003596334459461)
XLA Ops:
  7.2 0.7 all-gather.2.cloned.1.call-update
  7.9 1.2 copy.15
  9.1 1.5 broadcast_in_dim.37
  10.7 4.4 %all-to-all-start = ((bf16[4,256,1024]{1,2,0:T(8,128)(2,1)}), bf16[4,256,1024]{1,2,0:T(8,128)(2,1)S(1)}, u32[]{:S(2)}, u32[]{:S(2)}) async-start(bf16[4,256,1024]{1,2,0:T(8,128)(2,1)} %broadcast_in_dim.37), calls=%async_computation | async-start | bytes 4194304 | tf_op jit(solution)/shard_map/all_to_all | solution.py:12
  15.7 25.7 %all-to-all-done = bf16[4,256,1024]{1,2,0:T(8,128)(2,1)S(1)} async-done(((bf16[4,256,1024]{1,2,0:T(8,128)(2,1)}), bf16[4,256,1024]{1,2,0:T(8,128)(2,1)S(1)}, u32[]{:S(2)}, u32[]{:S(2)}) %all-to-all-start) | async-done | bytes 2097184 | tf_op jit(solution)/shard_map/all_to_all | solution.py:12
  41.4 54.0 %all-gather.2.cloned.1.call-done = bf16[4096,1024]{1,0:T(8,128)(2,1)} async-done(((bf16[64,1024]{1,0:T(8,128)(2,1)}), bf16[4096,1024]{1,0:T(8,128)(2,1)}) %all-gather.2.cloned.1.call-update) | async-done | bytes 8388624 | tf_op jit(solution)/shard_map/all_gather | solution.py:69
  95.4 12.7 %convolution_convert_fusion.1 = bf16[256,4096]{1,0:T(8,128)(2,1)} fusion(bf16[4096,1024]{1,0:T(8,128)(2,1)} %all-gather.2.cloned.1.call-done, bf16[256,4096]{0,1:T(8,128)(2,1)S(1)} %bitcast.72, s32[2,256,1024]{2,1,0:T(8,128)} %param.14, f32[1024]{0:T(1024)S(1)} %copy-done.4, f32[]{:T(128)} %bitcast.63), kind=kOutput, calls=%fused_computation.1 | convolution fusion | flops 4299161600 | bytes 22024704 | tf_op jit(solution)/shard_map/dot_general | solution.py:76
  108.1 3.1 %copy.25 = bf16[32,4,8,1024]{3,2,0,1:T(8,128)(2,1)} copy(bf16[32,4,8,1024]{3,2,1,0:T(8,128)(2,1)} %bitcast.73) | data formatting | bytes 4194304 | tf_op jit(solution)/shard_map/reshape | solution.py:28
  111.2 4.2 %all-to-all-start.1 = ((bf16[4,256,1024]{2,1,0:T(8,128)(2,1)}), bf16[4,256,1024]{2,1,0:T(8,128)(2,1)S(1)}, u32[]{:S(2)}, u32[]{:S(2)}) async-start(bf16[4,256,1024]{2,1,0:T(8,128)(2,1)} %bitcast.69), calls=%async_computation.1 | async-start | bytes 4194304 | tf_op jit(solution)/shard_map/all_to_all | solution.py:33
  115.4 0.7 dynamic_slice.9
  116.1 7.7 %fusion.34 = (s32[1,256,4096]{2,1,0:T(8,128)}, s32[1,256,4096]{2,1,0:T(8,128)}) fusion(s32[2,256,4096]{2,1,0:T(8,128)} %param.15), kind=kLoop, calls=%fused_computation.52 | loop fusion | bytes 16777216 | tf_op jit(solution)/shard_map/slice | solution.py:80
  123.8 18.4 %all-to-all-done.1 = bf16[4,256,1024]{2,1,0:T(8,128)(2,1)S(1)} async-done(((bf16[4,256,1024]{2,1,0:T(8,128)(2,1)}), bf16[4,256,1024]{2,1,0:T(8,128)(2,1)S(1)}, u32[]{:S(2)}, u32[]{:S(2)}) %all-to-all-start.1) | async-done | bytes 2097184 | tf_op jit(solution)/shard_map/all_to_all | solution.py:33
  142.6 2.0 fusion.24
  145.0 28.8 %all_to_all.25 = bf16[4,256,1024]{1,2,0:T(8,128)(2,1)S(1)} all-to-all(bf16[4,256,1024]{1,2,0:T(8,128)(2,1)S(1)} %broadcast_in_dim.38), channel_id=1, replica_groups=mesh['temp'=64,'mp'=4] {'mp'}, dimensions={0} | all-to-all | bytes 4194304 | tf_op jit(solution)/shard_map/all_to_all | solution.py:12
  173.7 6.5 %fusion.14 = bf16[256,1024]{1,0:T(8,128)(2,1)S(1)} fusion(bf16[256,4096]{0,1:T(8,128)(2,1)S(1)} %bitcast.74, bf16[4096,1024]{1,0:T(8,128)(2,1)} %all-gather.2.cloned.1.call-done, s32[2,256,1024]{2,1,0:T(8,128)S(1)} %copy-done.3, f32[1024]{0:T(1024)S(1)} %copy-done.4, f32[]{:T(128)} %bitcast.67), kind=kOutput, calls=%fused_computation.24 | convolution fusion | flops 2150629376 | bytes 12062724 | tf_op jit(solution)/shard_map/dot_general | solution.py:72
  180.3 2.4 convolution_convert_fusion
  182.9 27.2 %all_to_all.26 = bf16[4,256,1024]{2,1,0:T(8,128)(2,1)S(1)} all-to-all(bf16[4,256,1024]{2,1,0:T(8,128)(2,1)S(1)} %bitcast.70), channel_id=1, replica_groups=mesh['temp'=64,'mp'=4] {'mp'}, dimensions={0} | all-to-all | bytes 4194304 | tf_op jit(solution)/shard_map/all_to_all | solution.py:33
  210.5 2.0 fusion.25
  212.6 1.9 collective-permute-start.2
  214.5 5.8 %collective-permute-start = (bf16[256,1024]{1,0:T(8,128)(2,1)S(1)}, bf16[256,1024]{1,0:T(8,128)(2,1)S(1)}, u32[]{:S(2)}, u32[]{:S(2)}) collective-permute-start(bf16[256,1024]{1,0:T(8,128)(2,1)S(1)} %fusion.25), channel_id=1, source_target_pairs={{4,0},{8,4},{12,8},{16,12},{20,16},{24,20},{28,24},{32,28},{36,32}... | collective-permute-start | bytes 1572872 | tf_op jit(solution)/shard_map/ppermute | solution.py:40
  220.3 1.9 collective-permute-start.1
  222.3 5.0 %collective-permute-done.1 = bf16[256]{0:T(256)(128)(2,1)S(1)} collective-permute-done((bf16[256]{0:T(256)(128)(2,1)S(1)}, bf16[256]{0:T(256)(128)(2,1)S(1)}, u32[]{:S(2)}, u32[]{:S(2)}) %collective-permute-start.1) | collective-permute-done | bytes 544 | tf_op jit(solution)/shard_map/ppermute | solution.py:40
  228.0 1.5 broadcast_in_dim.40
  229.5 3.6 %all-to-all-start.4 = ((bf16[4,256,1024]{1,2,0:T(8,128)(2,1)}), bf16[4,256,1024]{1,2,0:T(8,128)(2,1)S(1)}, u32[]{:S(2)}, u32[]{:S(2)}) async-start(bf16[4,256,1024]{1,2,0:T(8,128)(2,1)} %broadcast_in_dim.40), calls=%async_computation.4 | async-start | bytes 4194304 | tf_op jit(solution)/shard_map/all_to_all | solution.py:12
  233.1 1.9 collective-permute-start.4
  235.0 5.8 %collective-permute-start.3 = (bf16[256,1024]{1,0:T(8,128)(2,1)S(1)}, bf16[256,1024]{1,0:T(8,128)(2,1)S(1)}, u32[]{:S(2)}, u32[]{:S(2)}) collective-permute-start(bf16[256,1024]{1,0:T(8,128)(2,1)S(1)} %fusion.14), channel_id=1, source_target_pairs={{4,0},{8,4},{12,8},{16,12},{20,16},{24,20},{28,24},{32,28},{36,32}... | collective-permute-start | bytes 1572872 | tf_op jit(solution)/shard_map/ppermute | solution.py:40
  240.8 4.9 %collective-permute-done.4 = bf16[256,1024]{1,0:T(8,128)(2,1)S(1)} collective-permute-done((bf16[256,1024]{1,0:T(8,128)(2,1)S(1)}, bf16[256,1024]{1,0:T(8,128)(2,1)S(1)}, u32[]{:S(2)}, u32[]{:S(2)}) %collective-permute-start.4) | collective-permute-done | bytes 524320 | tf_op jit(solution)/shard_map/ppermute | solution.py:40
  245.7 1.8 collective-permute-done.3
  247.5 0.9 select_select_fusion
  248.4 10.7 %all-to-all-done.4 = bf16[4,256,1024]{1,2,0:T(8,128)(2,1)S(1)} async-done(((bf16[4,256,1024]{1,2,0:T(8,128)(2,1)}), bf16[4,256,1024]{1,2,0:T(8,128)(2,1)S(1)}, u32[]{:S(2)}, u32[]{:S(2)}) %all-to-all-start.4) | async-done | bytes 2097184 | tf_op jit(solution)/shard_map/all_to_all | solution.py:12
  259.1 6.3 %fusion.15 = f32[256]{0:T(256)S(1)} fusion(bf16[256,4096]{0,1:T(8,128)(2,1)S(1)} %bitcast.71, bf16[4096,1024]{1,0:T(8,128)(2,1)} %all-gather.2.cloned.1.call-done, f32[1024]{0:T(1024)S(1)} %copy-done.4, f32[]{:T(128)} %bitcast.65), kind=kOutput, calls=%fused_computation.25 | convolution fusion | flops 2149842688 | bytes 10490884 | tf_op jit(solution)/shard_map/dot_general | solution.py:98
  265.5 9.5 %psum.7 = f32[256]{0:T(256)} all-reduce(f32[256]{0:T(256)S(1)} %negate_multiply_fusion), channel_id=1, replica_groups=mesh['temp'=64,'mp'=4] {'mp'}, use_global_device_ids=true, to_apply=%region_4.5 | all-reduce | flops 256 | bytes 2048 | tf_op jit(solution)/shard_map/psum | solution.py:102
  (28 shorter events, 2.0 us)
Async XLA Ops:
  7.2 88.2 %all-gather.2.cloned.1.call-start = ((), (), s32[]{:S(2)}) async-start(), calls=%async_computation.5 | async-start | bytes 8519680 | tf_op jit(solution)/shard_map/all_gather | solution.py:69
  10.7 84.7 %copy-start.4 = (f32[1024]{0:T(1024)S(1)}, f32[1024]{0:T(1024)}, u32[]{:S(2)}) copy-start(f32[1024]{0:T(1024)} %param.12) | copy-start | bytes 12292
  10.7 30.8 %all-to-all-start = ((bf16[4,256,1024]{1,2,0:T(8,128)(2,1)}), bf16[4,256,1024]{1,2,0:T(8,128)(2,1)S(1)}, u32[]{:S(2)}, u32[]{:S(2)}) async-start(bf16[4,256,1024]{1,2,0:T(8,128)(2,1)} %broadcast_in_dim.37), calls=%async_computation | async-start | bytes 4194304 | tf_op jit(solution)/shard_map/all_to_all | solution.py:12
  111.2 31.0 %all-to-all-start.1 = ((bf16[4,256,1024]{2,1,0:T(8,128)(2,1)}), bf16[4,256,1024]{2,1,0:T(8,128)(2,1)S(1)}, u32[]{:S(2)}, u32[]{:S(2)}) async-start(bf16[4,256,1024]{2,1,0:T(8,128)(2,1)} %bitcast.69), calls=%async_computation.1 | async-start | bytes 4194304 | tf_op jit(solution)/shard_map/all_to_all | solution.py:33
  144.8 28.9 %copy-start.3 = (s32[2,256,1024]{2,1,0:T(8,128)S(1)}, s32[2,256,1024]{2,1,0:T(8,128)}, u32[]{:S(2)}) copy-start(s32[2,256,1024]{2,1,0:T(8,128)} %param.14) | copy-start | bytes 6291460
  145.0 35.3 %slice-start = ((s8[8388608]{0:T(1024)(128)(4,1)}), s8[4194304]{0:T(1024)(128)(4,1)S(1)}, s32[]{:S(2)}) async-start(s8[8388608]{0:T(1024)(128)(4,1)} %bitcast.76), calls=%async_computation.6 | async-start | bytes 8388608
  173.7 6.5 %slice-start.1 = ((s8[8388608]{0:T(1024)(128)(4,1)}), s8[4194304]{0:T(1024)(128)(4,1)S(1)}, s32[]{:S(2)}) async-start(s8[8388608]{0:T(1024)(128)(4,1)} %bitcast.76), calls=%async_computation.7 | async-start | bytes 8388608
  210.5 9.8 %copy-start.1 = (s32[256]{0:T(256)S(1)}, s32[256]{0:T(256)}, u32[]{:S(2)}) copy-start(s32[256]{0:T(256)} %param.17) | copy-start | bytes 3076
  210.5 16.8 %copy-start.2 = (s32[256]{0:T(256)S(1)}, s32[256]{0:T(256)}, u32[]{:S(2)}) copy-start(s32[256]{0:T(256)} %param.16) | copy-start | bytes 3076
  212.6 14.7 %collective-permute-start.2 = (bf16[256,1024]{1,0:T(8,128)(2,1)S(1)}, bf16[256,1024]{1,0:T(8,128)(2,1)S(1)}, u32[]{:S(2)}, u32[]{:S(2)}) collective-permute-start(bf16[256,1024]{1,0:T(8,128)(2,1)S(1)} %fusion.25), channel_id=1, source_target_pairs={{0,4},{4,8},{8,12},{12,16},{16,20},{20,24},{24,28},{28,32},{32,36}... | collective-permute-start | bytes 1572872 | tf_op jit(solution)/shard_map/ppermute | solution.py:40
  214.5 12.8 %collective-permute-start = (bf16[256,1024]{1,0:T(8,128)(2,1)S(1)}, bf16[256,1024]{1,0:T(8,128)(2,1)S(1)}, u32[]{:S(2)}, u32[]{:S(2)}) collective-permute-start(bf16[256,1024]{1,0:T(8,128)(2,1)S(1)} %fusion.25), channel_id=1, source_target_pairs={{4,0},{8,4},{12,8},{16,12},{20,16},{24,20},{28,24},{32,28},{36,32}... | collective-permute-start | bytes 1572872 | tf_op jit(solution)/shard_map/ppermute | solution.py:40
  220.3 7.0 %collective-permute-start.1 = (bf16[256]{0:T(256)(128)(2,1)S(1)}, bf16[256]{0:T(256)(128)(2,1)S(1)}, u32[]{:S(2)}, u32[]{:S(2)}) collective-permute-start(bf16[256]{0:T(256)(128)(2,1)S(1)} %convert_element_type.58), channel_id=1, source_target_pairs={{0,4},{4,8},{8,12},{12,16},{16,20},{20,24},{24,28},{28,32},{32,36}... | collective-permute-start | bytes 1544 | tf_op jit(solution)/shard_map/ppermute | solution.py:40
  227.8 1.7 copy-start
  229.5 29.6 %all-to-all-start.4 = ((bf16[4,256,1024]{1,2,0:T(8,128)(2,1)}), bf16[4,256,1024]{1,2,0:T(8,128)(2,1)S(1)}, u32[]{:S(2)}, u32[]{:S(2)}) async-start(bf16[4,256,1024]{1,2,0:T(8,128)(2,1)} %broadcast_in_dim.40), calls=%async_computation.4 | async-start | bytes 4194304 | tf_op jit(solution)/shard_map/all_to_all | solution.py:12
  233.1 12.6 %collective-permute-start.4 = (bf16[256,1024]{1,0:T(8,128)(2,1)S(1)}, bf16[256,1024]{1,0:T(8,128)(2,1)S(1)}, u32[]{:S(2)}, u32[]{:S(2)}) collective-permute-start(bf16[256,1024]{1,0:T(8,128)(2,1)S(1)} %fusion.14), channel_id=1, source_target_pairs={{0,4},{4,8},{8,12},{12,16},{16,20},{20,24},{24,28},{28,32},{32,36}... | collective-permute-start | bytes 1572872 | tf_op jit(solution)/shard_map/ppermute | solution.py:40
  235.0 12.4 %collective-permute-start.3 = (bf16[256,1024]{1,0:T(8,128)(2,1)S(1)}, bf16[256,1024]{1,0:T(8,128)(2,1)S(1)}, u32[]{:S(2)}, u32[]{:S(2)}) collective-permute-start(bf16[256,1024]{1,0:T(8,128)(2,1)S(1)} %fusion.14), channel_id=1, source_target_pairs={{4,0},{8,4},{12,8},{16,12},{20,16},{24,20},{28,24},{32,28},{36,32}... | collective-permute-start | bytes 1572872 | tf_op jit(solution)/shard_map/ppermute | solution.py:40
Sparse Core Ops, SparseCore 0:
  10.8 84.5 all-gather.1
where the time goes:
time: 283 us; the launch traced here: 282 us
  waiting for transfers between devices  121 us (43%)
  blocking collectives  65.4 us (23%)
  starting transfers between devices  29.6 us (10%)
  matrix products  27.9 us (10%)
  local copies, waits for them, and re-layouts  16.6 us (6%)
  between operations  14.9 us (5%)
  other arithmetic  6.24 us (2%)
    all_gather x1, waiting for transfers between devices, on_device(): weight_cols = lax.all_gather(weights, 'temp', axis=0, tiled=True)  54 us
    all_to_all x2, waiting for transfers between devices, copy_for_each(): return lax.all_to_all(copies, axis, split_axis=0, concat_axis=0, tiled=True)  36.4 us
    all_to_all x1, blocking collectives, copy_for_each(): return lax.all_to_all(copies, axis, split_axis=0, concat_axis=0, tiled=True)  28.8 us
    all_to_all x1, blocking collectives, sent_and_summed(): lax.all_to_all(pieces, axis, split_axis=0, concat_axis=0, tiled=True)  27.2 us
    all_to_all x1, waiting for transfers between devices, sent_and_summed(): lax.all_to_all(pieces, axis, split_axis=0, concat_axis=0, tiled=True)  18.4 us
    ppermute x5, starting transfers between devices, from_behind(): lax.ppermute(value, axis, [(source, source + steps) for source in range(f...  17.3 us
    dot_general x2, matrix products, on_device(): lax.dot_general(hidden, weight_cols, (((1,), (1,)), ((), ())), preferred_...  15.1 us
    ppermute x5, waiting for transfers between devices, from_behind(): lax.ppermute(value, axis, [(source, source + steps) for source in range(f...  11.7 us
  transfers between devices with their start and end apart: 9, of which 7 were waited for; matrix products, arithmetic and copies ran while one was open for 4% of the time, Pallas kernels for 0%

commit v1 on v0

v1 whole, which is shorter than its diff:
```python
import heapq

import jax
import jax.numpy as jnp
from jax import lax
from jax.experimental import pallas as pl
from jax.experimental.pallas import tpu as pltpu
from jax.sharding import PartitionSpec as P

NH = 4096
SWEEPS = 2
NY, NZ, NX, NT = 4, 8, 4, 64
ROWS, BLK, CW = 256, 1024, 256
F32, BF16 = jnp.float32, jnp.bfloat16
MESH = pl.DeviceIdType.MESH


def gather_plan():
    msgs = []
    for s in (1, -1):
        for d in range(1, 5):
            first, rows = (32, 32) if d < 4 else ((32, 16) if s > 0 else (48, 16))
            msgs.append((("BZ", s, d), (0, 0, s), (0, 0, -s * (d - 1)), first, rows, [("BZ", s, d - 1)] if d > 1 else []))
    msgs.append((("AY", 1, 1), (0, 1, 0), (0, 0, 0), 0, 32, []))
    msgs.append((("AY", -1, 1), (0, -1, 0), (0, 0, 0), 0, 32, []))
    msgs.append((("AY", 1, 2), (0, 1, 0), (0, -1, 0), 0, 16, [("AY", 1, 1)]))
    msgs.append((("AY", -1, 2), (0, -1, 0), (0, 1, 0), 16, 16, [("AY", -1, 1)]))
    there = ([], [("AY", 1, 1)], [("AY", -1, 1)], [("AY", 1, 2), ("AY", -1, 2)])
    for d in range(1, 5):
        for j, oy in enumerate((0, -1, 1, 2)):
            for s in (1, -1):
                if d == 4 and (j < 2) != (s > 0):
                    continue
                deps = there[j] if d == 1 else [("AZ", s, d - 1, j)]
                msgs.append((("AZ", s, d, j), (0, 0, s), (0, oy, -s * (d - 1)), 0, 32, deps))
    for zz in (0, -1, 1, -2, 2, -3, 3, 4):
        deps = [] if zz == 0 else ([("BZ", 1, 4), ("BZ", -1, 4)] if zz == 4 else [("BZ", -1 if zz > 0 else 1, abs(zz))])
        for s in (1, -1):
            msgs.append((("BY", s, 1, zz), (0, s, 0), (0, 0, zz), 32, 32, deps))
        s = 1 if zz in (0, 1, -2, 3) else -1
        msgs.append((("BY", s, 2, zz), (0, s, 0), (0, -s, zz), 32, 32, [("BY", s, 1, zz)]))
    for s in (1, -1):
        for j in (0, 2, 1, 3):
            msgs.append((("AX", s, 1, j), (s, 0, 0), (0, 0, 0), j, 4, []))
        for j in ((0, 1) if s > 0 else (2, 3)):
            msgs.append((("AX", s, 2, j), (s, 0, 0), (-s, 0, 0), j, 4, [("AX", s, 1, j)]))
    return msgs


def arrival_order(msgs):
    free, done, left = {}, set(), {m[0]: m for m in msgs}
    order, events, first = [], [], []

    def issue(now):
        for name in [n for n, m in left.items() if all(d in done for d in m[5])]:
            m = left.pop(name)
            cost = m[4] / 32 * (1.4 if m[1][0] == 0 else 0.7 * 32 / 4 * 4 / 8)
            begin = max(now, free.get(m[1], 0.0))
            free[m[1]] = begin + cost
            heapq.heappush(events, (begin + cost + 2.0, len(order), name))
            order.append((name, now))

    issue(0.0)
    sends = {None: [n for n, _ in order]}
    waits = []
    while events:
        now, _, name = heapq.heappop(events)
        done.add(name)
        waits.append(name)
        before = len(order)
        issue(now)
        sends[name] = [n for n, _ in order[before:]]
    return sends, waits


MSGS = gather_plan()
INDEX = {m[0]: i for i, m in enumerate(MSGS)}
SENDS, WAITS = arrival_order(MSGS)


def kernel(
    chains, weights, vbias, hbias, temps, hthr, vthr, phase, accept,
    vis_out, hid_out, energy_out,
    W, V, thr, L, acc, H, SB, RB, PF, meta, metar, swapv, swaph, vo, ho, BT, TU, TL, ebuf,
    gs, gr, dsem, ags, agr, rss, rsr, sws, swr, ms, mr, es, er, lsem,
):
    t = lax.axis_index("temp")
    m = lax.axis_index("mp")
    c = lax.rem(t, 2)
    z = lax.rem(t // 2, NZ)
    y = t // (2 * NZ)

    def col(d):
        return lax.rem(m + d + NX, NX)

    def rep(d):
        return lax.rem(t + d + NT, NT)

    def temp_of(dy, dz):
        return (lax.rem(y + dy + NY, NY) * NZ + lax.rem(z + dz + NZ, NZ)) * 2 + c

    pending = []

    def send(src, dst, ssem, rsem, device):
        copy = pltpu.make_async_remote_copy(
            src_ref=src, dst_ref=dst, send_sem=ssem, recv_sem=rsem, device_id=device, device_id_type=MESH
        )
        copy.start()
        return copy

    def arrived(ref, sem):
        pltpu.make_async_copy(ref, ref, sem).wait()

    wload = pltpu.make_async_copy(weights, W.at[pl.ds(pl.multiple_of(t * 64, 64), 64)], lsem.at[0])
    wload.start()
    vload = []
    for j in range(4):
        cp = pltpu.make_async_copy(chains.at[:, pl.ds(j * CW, CW)], V.at[0, 4 * m + j], lsem.at[1 + j])
        cp.start()
        vload.append(cp)
    tload = []
    for s in range(SWEEPS):
        cp = pltpu.make_async_copy(hthr.at[s], thr.at[2 * s], lsem.at[5 + 2 * s])
        cp.start()
        tload.append(cp)
        cp = pltpu.make_async_copy(
            vthr.at[s, :, pl.ds(pl.multiple_of(m * BLK, BLK), BLK)], thr.at[2 * s + 1], lsem.at[6 + 2 * s]
        )
        cp.start()
        tload.append(cp)
    beta = temps[0:1, 0:1]
    meta[...] = jnp.broadcast_to(beta, (8, 128))
    meta[0:2, :] = accept[...].astype(F32)

    barrier = pltpu.get_barrier_semaphore()
    peers = [(t, col(d)) for d in (1, 2, 3)]
    peers += [(rep(e), col(d)) for e in (1, -1) for d in range(4)]
    peers += [(temp_of(1, 0), m), (temp_of(-1, 0), m), (temp_of(0, 1), m), (temp_of(0, -1), m)]
    for p in peers:
        pl.semaphore_signal(barrier, inc=1, device_id=p, device_id_type=MESH)
    pl.semaphore_wait(barrier, len(peers))

    sibling = (t + 1 - 2 * c, m)

    def rows_of(oy, oz, first, rows):
        start = temp_of(oy, oz) * 64 + first
        return W.at[pl.ds(pl.multiple_of(start, 16), rows)]

    def place(msg, seen):
        name, (sx, sy, sz), (ox, oy, oz), first, rows, _ = msg
        if sx:
            return V.at[0, 4 * col(ox - (sx if seen else 0)) + first]
        return rows_of(oy - (sy if seen else 0), oz - (sz if seen else 0), first, rows)

    def launch(name):
        msg = MSGS[INDEX[name]]
        sx, sy, sz = msg[1]
        ref = place(msg, False)
        device = (t, col(sx)) if sx else (temp_of(sy, sz), m)
        i = INDEX[name]
        pending.append(send(ref, ref, gs.at[i], gr.at[i], device))

    def to_sibling(ref):
        send(ref, ref, dsem.at[0], dsem.at[1], sibling)

    wload.wait()
    for name in SENDS[None]:
        if name[0] != "AX":
            launch(name)
    to_sibling(W.at[pl.ds(pl.multiple_of(t * 64, 64), 64)])
    for cp in vload:
        cp.wait()
    for name in SENDS[None]:
        if name[0] == "AX":
            launch(name)
    for e in (0, 1):
        pending.append(send(meta, metar.at[e], ms.at[e], mr.at[e], (rep(1 - 2 * e), m)))

    def prepare(k):
        tload[k].wait()

        def some(i, carry):
            r = pl.ds(pl.multiple_of(i * 32, 32), 32)
            level = (thr[k, r, :].astype(F32) + 0.5) / 256.0
            bias = hbias[...] if k % 2 == 0 else vbias[m]
            L[k, r, :] = beta * bias + (jnp.log(level) - jnp.log(1.0 - level))
            return carry

        lax.fori_loop(0, ROWS // 32, some, 0)

    def decisions():
        for e in (0, 1):
            arrived(metar.at[e], mr.at[e])
        low, up = metar.at[0], metar.at[1]
        ph = phase[...]
        lower = (lax.rem(t, 2) == ph) & (t + 1 < NT)
        upper = (lax.rem(t + 1, 2) == ph) & (t >= 1)
        take_up = jnp.where(lower & (accept[...] == 1), 1.0, 0.0)
        take_low = jnp.where(upper & (low[0:2, :] > 0.5), 1.0, 0.0)
        b = jnp.where(take_up > 0.5, up[2:4, :], jnp.where(take_low > 0.5, low[2:4, :], jnp.broadcast_to(beta, (2, 128))))
        for h in (0, 1):
            for ref, rows in ((TU, take_up), (TL, take_low), (BT, b)):
                ref[128 * h : 128 * h + 128, :] = jnp.broadcast_to(rows[h : h + 1, :], (128, 128)).T
        return take_up, take_low

    extra = {4: 0, 8: 1, 12: 2, 16: 3}
    flags = None
    for n, name in enumerate(WAITS):
        msg = MSGS[INDEX[name]]
        ref = place(msg, True)
        arrived(ref, gr.at[INDEX[name]])
        for nxt in SENDS[name]:
            launch(nxt)
        if name[0] != "AX":
            to_sibling(ref)
        if n in extra:
            prepare(extra[n])
        if n == 20:
            flags = decisions()
    take_up, take_low = flags
    half = W.at[pl.ds(0, NT // 2 * 64)]
    arrived(half, dsem.at[1])

    def dot(a, b):
        return jnp.dot(a, b, preferred_element_type=F32)

    def wtile(b, j, n, width):
        return W[pl.ds(pl.multiple_of(b * BLK + j * CW, CW), CW), pl.ds(pl.multiple_of(n * width, width), width)]

    def add_product(a, blocks, fresh):
        def tile(n, carry):
            cols = pl.ds(pl.multiple_of(n * 256, 256), 256)
            total = None
            for b, j in blocks:
                part = dot(V[a, 4 * b + j], wtile(b, j, n, 256))
                total = part if total is None else total + part
            acc[:, cols] = total if fresh else acc[:, cols] + total
            return carry

        lax.fori_loop(0, 4, tile, 0)

    def gathered_product(a):
        add_product(a, [(m, j) for j in range(4)], True)
        for j in (0, 2, 1, 3):
            arrived(V.at[a, 4 * col(-1) + j], agr.at[a - 1, j])
            if j < 2:
                ref = V.at[a, 4 * col(-1) + j]
                pending.append(send(ref, ref, ags.at[a - 1, 4 + j], agr.at[a - 1, 4 + j], (t, col(1))))
            arrived(V.at[a, 4 * col(1) + j], agr.at[a - 1, 6 + j])
            if j >= 2:
                ref = V.at[a, 4 * col(1) + j]
                pending.append(send(ref, ref, ags.at[a - 1, 8 + j], agr.at[a - 1, 8 + j], (t, col(-1))))
            add_product(a, [(col(-1), j), (col(1), j)], False)
        for f in (0, 1):
            arrived(V.at[a, 4 * col(2) + f], agr.at[a - 1, 4 + f])
            arrived(V.at[a, 4 * col(2) + 2 + f], agr.at[a - 1, 10 + f])
            add_product(a, [(col(2), f), (col(2), 2 + f)], False)

    def hidden_states(s):
        def tile(n, carry):
            cols = pl.ds(pl.multiple_of(n * 256, 256), 256)
            H[s, :, cols] = jax.nn.sigmoid(beta * acc[:, cols] + L[2 * s, :, cols]).astype(BF16)
            return carry

        lax.fori_loop(0, 4, tile, 0)

    def partial(s, b, j):
        return lax.dot_general(
            H[s], W[pl.ds(pl.multiple_of(b * BLK + j * CW, CW), CW), :], (((1,), (1,)), ((), ())),
            preferred_element_type=F32,
        )

    def order(i):
        return lax.rem(2 * i, 4) + lax.rem(i, 4) // 2

    def visible_states(s):
        def first(i, carry):
            g, j = i // 4, order(i)
            sg = 1 - 2 * (j // 2)
            b = jnp.where(g == 0, col(2), col(-sg))
            target = jnp.where(g == 0, col(sg), col(-sg))
            k = 4 * g + j
            SB[s, k] = partial(s, b, j).astype(BF16)
            send(SB.at[s, k], RB.at[s, k], rss.at[s, k], rsr.at[s, k], (t, target))
            return carry

        lax.fori_loop(0, 8, first, 0)

        def merge(i, carry):
            j = order(i)
            sg = 1 - 2 * (j // 2)
            term = partial(s, col(sg), j)
            arrived(RB.at[s, j], rsr.at[s, j])
            SB[s, 8 + j] = (term + RB[s, j].astype(F32)).astype(BF16)
            send(SB.at[s, 8 + j], RB.at[s, 8 + j], rss.at[s, 8 + j], rsr.at[s, 8 + j], (t, col(sg)))
            return carry

        lax.fori_loop(0, 4, merge, 0)

        def own(j, carry):
            PF[j] = partial(s, m, j)
            return carry

        lax.fori_loop(0, 4, own, 0)

        def last(i, carry):
            j = order(i)
            arrived(RB.at[s, 4 + j], rsr.at[s, 4 + j])
            arrived(RB.at[s, 8 + j], rsr.at[s, 8 + j])
            pre = PF[j] + RB[s, 4 + j].astype(F32) + RB[s, 8 + j].astype(F32)
            cols = pl.ds(pl.multiple_of(j * CW, CW), CW)
            V[s + 1, 4 * m + j] = jax.nn.sigmoid(beta * pre + L[2 * s + 1, :, cols]).astype(BF16)
            ref = V.at[s + 1, 4 * m + j]
            send(ref, ref, ags.at[s, j], agr.at[s, j], (t, col(1)))
            send(ref, ref, ags.at[s, 6 + j], agr.at[s, 6 + j], (t, col(-1)))
            return carry

        lax.fori_loop(0, 4, last, 0)

    add_product(0, [(b, j) for b in range(4) for j in range(4)], True)
    hidden_states(0)
    visible_states(0)
    gathered_product(1)
    hidden_states(1)
    for e in (0, 1):
        pending.append(send(H.at[1], swaph.at[e], sws.at[e], swr.at[e], (rep(1 - 2 * e), m)))
    visible_states(1)
    mine = V.at[2, pl.ds(4 * m, 4)]
    for e in (0, 1):
        pending.append(send(mine, swapv.at[e], sws.at[2 + e], swr.at[2 + e], (rep(1 - 2 * e), m)))

    gathered_product(2)

    def bias_part(g, total):
        return total + V[2, 4 * m + g // 2, :, pl.ds(pl.multiple_of(lax.rem(g, 2) * 128, 128), 128)].astype(F32) * vbias[
            m, :, pl.ds(pl.multiple_of(g * 128, 128), 128)
        ]

    total = BT[...] * lax.fori_loop(0, 8, bias_part, jnp.zeros((ROWS, 128), F32))

    def soft_part(g, total):
        cols = pl.ds(pl.multiple_of(g * 128, 128), 128)
        x = BT[...] * (acc[:, cols] + hbias[:, cols])
        return total + (jnp.maximum(x, 0.0) + jnp.log1p(jnp.exp(-jnp.abs(x))))

    total = lax.fori_loop(0, 8, soft_part, total)
    ebuf[0, m] = jnp.zeros((8, 128), F32)
    for h in (0, 1):
        ebuf[0, m, h : h + 1, :] = jnp.sum(total[128 * h : 128 * h + 128, :].T, axis=0, keepdims=True) * (-1.0 / NH)
    targets = [(0, d) for d in (1, 2, 3)] + [(e, d) for e in (1, -1) for d in range(4)]
    for e, d in targets:
        i = (e % 3) * 4 + d
        pending.append(send(ebuf.at[0, m], ebuf.at[e % 3, m], es.at[i], er.at[i], (rep(e), col(d))))

    for e in (0, 1):
        arrived(swaph.at[e], swr.at[e])

    def swap_hidden(g, carry):
        cols = pl.ds(pl.multiple_of(g * 128, 128), 128)
        low, up, own = swaph[0, :, cols].astype(F32), swaph[1, :, cols].astype(F32), H[1, :, cols].astype(F32)
        ho[:, cols] = jnp.where(TU[...] > 0.5, up, jnp.where(TL[...] > 0.5, low, own)).astype(BF16)
        return carry

    lax.fori_loop(0, 8, swap_hidden, 0)
    hput = pltpu.make_async_copy(ho, hid_out, lsem.at[9])
    hput.start()
    for e in (0, 1):
        arrived(swapv.at[e], swr.at[2 + e])

    def swap_visible(g, carry):
        cols = pl.ds(pl.multiple_of(lax.rem(g, 2) * 128, 128), 128)
        k = g // 2
        low, up = swapv[0, k, :, cols].astype(F32), swapv[1, k, :, cols].astype(F32)
        own = V[2, 4 * m + k, :, cols].astype(F32)
        vo[:, pl.ds(pl.multiple_of(g * 128, 128), 128)] = jnp.where(
            TU[...] > 0.5, up, jnp.where(TL[...] > 0.5, low, own)
        ).astype(BF16)
        return carry

    lax.fori_loop(0, 8, swap_visible, 0)
    vput = pltpu.make_async_copy(vo, vis_out, lsem.at[10])
    vput.start()
    for e, d in targets:
        arrived(ebuf.at[e % 3, col(-d)], er.at[(e % 3) * 4 + d])

    def summed(k):
        return ebuf[k, 0, 0:2, :] + ebuf[k, 1, 0:2, :] + ebuf[k, 2, 0:2, :] + ebuf[k, 3, 0:2, :]

    energy_out[...] = jnp.where(take_up > 0.5, summed(2), jnp.where(take_low > 0.5, summed(1), summed(0)))

    for copy in pending:
        copy.wait_send()
    arrived(half, dsem.at[0])
    for s in range(SWEEPS):

        def left(k, carry):
            arrived(SB.at[s, k], rss.at[s, k])
            return carry

        lax.fori_loop(0, 12, left, 0)
        for j in range(4):
            arrived(V.at[s + 1, j], ags.at[s, j])
            arrived(V.at[s + 1, j], ags.at[s, 6 + j])
    hput.wait()
    vput.wait()


def on_device(
    chains, weights, visible_bias, hidden_bias, inv_temps, hidden_thresholds, visible_thresholds, swap_phase, swap_accept
):
    vmem = pl.BlockSpec(memory_space=pltpu.VMEM)
    hbm = pl.BlockSpec(memory_space=pl.ANY)
    dma = pltpu.SemaphoreType.DMA
    n = len(MSGS)
    vis, hid, energy = pl.pallas_call(
        kernel,
        out_shape=(
            jax.ShapeDtypeStruct((ROWS, BLK), BF16),
            jax.ShapeDtypeStruct((ROWS, BLK), BF16),
            jax.ShapeDtypeStruct((2, 128), F32),
        ),
        in_specs=[hbm, hbm, vmem, vmem, vmem, hbm, hbm, vmem, vmem],
        out_specs=(hbm, hbm, vmem),
        scratch_shapes=[
            pltpu.VMEM((4096, BLK), BF16),
            pltpu.VMEM((3, 16, ROWS, CW), BF16),
            pltpu.VMEM((4, ROWS, BLK), jnp.int32),
            pltpu.VMEM((4, ROWS, BLK), F32),
            pltpu.VMEM((ROWS, BLK), F32),
            pltpu.VMEM((2, ROWS, BLK), BF16),
            pltpu.VMEM((2, 12, ROWS, CW), BF16),
            pltpu.VMEM((2, 12, ROWS, CW), BF16),
            pltpu.VMEM((4, ROWS, CW), F32),
            pltpu.VMEM((8, 128), F32),
            pltpu.VMEM((2, 8, 128), F32),
            pltpu.VMEM((2, 4, ROWS, CW), BF16),
            pltpu.VMEM((2, ROWS, BLK), BF16),
            pltpu.VMEM((ROWS, BLK), BF16),
            pltpu.VMEM((ROWS, BLK), BF16),
            pltpu.VMEM((ROWS, 128), F32),
            pltpu.VMEM((ROWS, 128), F32),
            pltpu.VMEM((ROWS, 128), F32),
            pltpu.VMEM((3, 4, 8, 128), F32),
            dma((n,)), dma((n,)), dma((2,)),
            dma((2, 12)), dma((2, 12)), dma((2, 12)), dma((2, 12)),
            dma((4,)), dma((4,)), dma((2,)), dma((2,)), dma((12,)), dma((12,)), dma((11,)),
        ],
        compiler_params=pltpu.CompilerParams(
            collective_id=0, has_side_effects=True, vmem_limit_bytes=58 * 2**20
        ),
        name="tempered",
    )(
        chains,
        weights,
        visible_bias.reshape(4, 1, BLK),
        hidden_bias.reshape(1, BLK),
        inv_temps.reshape(1, 1),
        hidden_thresholds,
        visible_thresholds,
        swap_phase.reshape(2, 128),
        swap_accept.reshape(2, 128),
    )
    return vis, hid, energy.reshape(ROWS)


def solution(mesh):
    return jax.shard_map(
        on_device,
        mesh=mesh,
        in_specs=(
            P("temp", "mp"),
            P("temp", "mp"),
            P(),
            P("mp"),
            P("temp"),
            P(None, "temp", "mp"),
            P(None, "temp", None),
            P(),
            P("temp"),
        ),
        out_specs=(P("temp", "mp"), P("temp", "mp"), P("temp")),
        check_vma=False,
    )
```

time: 283 us -> 144 us (0.51)
  Pallas kernels: 0 us -> 136 us
  waiting for transfers between devices: 121 us -> 0 us
  blocking collectives: 65.4 us -> 0 us
  starting transfers between devices: 29.6 us -> 0 us
  matrix products: 27.9 us -> 0 us
  between operations: 14.9 us -> 1.29 us
  local copies, waits for them, and re-layouts: 16.6 us -> 4.98 us
  other arithmetic: 6.24 us -> 0 us
    pallas_call x0 -> x1, Pallas kernels: none -> 136 us  [on_device(): pl.pallas_call(kernel, out_shape=(jax.ShapeDtypeStruct((ROWS, BLK), BF16)...]
    all_to_all x2 -> x0, blocking collectives: 55.9 us -> none  [the longest x1 28.8 us: copy_for_each(): return lax.all_to_all(copies, axis, split_axis=0, concat_axis=0, tiled=True)]
    all_to_all x3 -> x0, waiting for transfers between devices: 54.7 us -> none  [the longest x2 36.4 us: copy_for_each(): return lax.all_to_all(copies, axis, split_axis=0, concat_axis=0, tiled=True)]
    all_gather x1 -> x0, waiting for transfers between devices: 54 us -> none  [on_device(): weight_cols = lax.all_gather(weights, 'temp', axis=0, tiled=True)]
    dot_general x4 -> x0, matrix products: 27.9 us -> none  [the longest x2 15.1 us: on_device(): lax.dot_general(hidden, weight_cols, (((1,), (1,)), ((), ())), preferred_...]
    ppermute x5 -> x0, starting transfers between devices: 17.3 us -> none  [from_behind(): lax.ppermute(value, axis, [(source, source + steps) for source in range(f...]
    all_to_all x3 -> x0, starting transfers between devices: 12.3 us -> none  [the longest x2 8.03 us: copy_for_each(): return lax.all_to_all(copies, axis, split_axis=0, concat_axis=0, tiled=True)]
    ppermute x5 -> x0, waiting for transfers between devices: 11.7 us -> none  [from_behind(): lax.ppermute(value, axis, [(source, source + steps) for source in range(f...]
  transfers between devices with their start and end apart: 9 -> 0, of which waited for: 7 -> 0; matrix products, arithmetic and copies ran while one was open for 4% -> 0% of each run, Pallas kernels for 0% -> 0%
where the time goes in v1:
time: 144 us; the launch traced here: 142 us
  Pallas kernels  136 us (94%)
  local copies, waits for them, and re-layouts  4.98 us (3%)
    pallas_call x1, Pallas kernels, on_device(): pl.pallas_call(kernel, out_shape=(jax.ShapeDtypeStruct((ROWS, BLK), BF16)...  136 us
    unnamed x3, local copies, waits for them, and re-layouts  4.98 us

profile of v1, /device:TPU:8, one launch (start us, length us, event | category | flops | bytes accessed | tf_op | source)
XLA Modules:
  0.0 142.4 jit_solution(3868141499738335964)
XLA Ops:
  1.3 136.2 %tempered.1 = (bf16[256,1024]{1,0:T(8,128)(2,1)}, bf16[256,1024]{1,0:T(8,128)(2,1)}, f32[2,128]{1,0:T(2,128)}) custom-call(bf16[256,1024]{1,0:T(8,128)(2,1)} %chains.1, bf16[64,1024]{1,0:T(8,128)(2,1)} %weights.1, f32[4,1,1024]{2,1,0:T(1,128)} %bitcast.7, f32[1,1024]{1,0:T(1,128)} %bitcast.8, f32[1,1]{1,0:T(1,128)} %bitcast.6.temps, s32[2,256,1024]{2,1,0:T(8,128)} %hthr.1, ...), custom_call_target="tpu_custom_call" | custom-call | tf_op jit(solution)/shard_map/tempered/pallas_call | solution.py:415
  137.5 1.9 %copy.16 = bf16[256,1024]{1,0:T(8,128)(2,1)} copy(bf16[256,1024]{1,0:T(8,128)(2,1)} %get-tuple-element.12) | data formatting | bytes 1048576
  139.3 1.9 %copy.17 = bf16[256,1024]{1,0:T(8,128)(2,1)} copy(bf16[256,1024]{1,0:T(8,128)(2,1)} %get-tuple-element.13) | data formatting | bytes 1048576
  141.2 1.2 copy.18

commit v2 on v1

--- a/solution.py
+++ b/solution.py
@@ -54,7 +54,7 @@
     def issue(now):
         for name in [n for n, m in left.items() if all(d in done for d in m[5])]:
             m = left.pop(name)
-            cost = m[4] / 32 * (1.4 if m[1][0] == 0 else 0.7 * 32 / 4 * 4 / 8)
+            cost = 2.8 if m[1][0] else 1.4 * m[4] / 32
             begin = max(now, free.get(m[1], 0.0))
             free[m[1]] = begin + cost
             heapq.heappush(events, (begin + cost + 2.0, len(order), name))
@@ -133,8 +133,7 @@
     meta[0:2, :] = accept[...].astype(F32)
 
     barrier = pltpu.get_barrier_semaphore()
-    peers = [(t, col(d)) for d in (1, 2, 3)]
-    peers += [(rep(e), col(d)) for e in (1, -1) for d in range(4)]
+    peers = [(t, col(1)), (t, col(-1)), (rep(1), m), (rep(-1), m)]
     peers += [(temp_of(1, 0), m), (temp_of(-1, 0), m), (temp_of(0, 1), m), (temp_of(0, -1), m)]
     for p in peers:
         pl.semaphore_signal(barrier, inc=1, device_id=p, device_id_type=MESH)

time: 144 us -> 134 us (0.931)
  Pallas kernels: 136 us -> 127 us
    pallas_call x1, Pallas kernels: 136 us -> 127 us  [on_device(): pl.pallas_call(kernel, out_shape=(jax.ShapeDtypeStruct((ROWS, BLK), BF16)...]
where the time goes in v2:
time: 134 us; the launch traced here: 133 us
  Pallas kernels  127 us (95%)
  local copies, waits for them, and re-layouts  4.98 us (4%)
    pallas_call x1, Pallas kernels, on_device(): pl.pallas_call(kernel, out_shape=(jax.ShapeDtypeStruct((ROWS, BLK), BF16)...  127 us
    unnamed x3, local copies, waits for them, and re-layouts  4.98 us

profile of v2, /device:TPU:8, one launch (start us, length us, event | category | flops | bytes accessed | tf_op | source)
XLA Modules:
  0.0 132.9 jit_solution(3097777505330356948)
XLA Ops:
  1.3 126.7 %tempered.1 = (bf16[256,1024]{1,0:T(8,128)(2,1)}, bf16[256,1024]{1,0:T(8,128)(2,1)}, f32[2,128]{1,0:T(2,128)}) custom-call(bf16[256,1024]{1,0:T(8,128)(2,1)} %chains.1, bf16[64,1024]{1,0:T(8,128)(2,1)} %weights.1, f32[4,1,1024]{2,1,0:T(1,128)} %bitcast.7, f32[1,1024]{1,0:T(1,128)} %bitcast.8, f32[1,1]{1,0:T(1,128)} %bitcast.6.temps, s32[2,256,1024]{2,1,0:T(8,128)} %hthr.1, ...), custom_call_target="tpu_custom_call" | custom-call | tf_op jit(solution)/shard_map/tempered/pallas_call | solution.py:414
  127.9 1.9 %copy.16 = bf16[256,1024]{1,0:T(8,128)(2,1)} copy(bf16[256,1024]{1,0:T(8,128)(2,1)} %get-tuple-element.12) | data formatting | bytes 1048576
  129.8 1.9 %copy.17 = bf16[256,1024]{1,0:T(8,128)(2,1)} copy(bf16[256,1024]{1,0:T(8,128)(2,1)} %get-tuple-element.13) | data formatting | bytes 1048576
  131.7 1.2 copy.18

commit v3 on v0

v3 whole, which is shorter than its diff:
```python
import heapq

import jax
import jax.numpy as jnp
from jax import lax
from jax.experimental import pallas as pl
from jax.experimental.pallas import tpu as pltpu
from jax.sharding import PartitionSpec as P

NH = 4096
SWEEPS = 2
NY, NZ, NX, NT = 4, 8, 4, 64
ROWS, HALF, BLK, CW = 256, 128, 1024, 256
F32, BF16, I32 = jnp.float32, jnp.bfloat16, jnp.int32
MESH = pl.DeviceIdType.MESH
FIRST = (24, 24)


def gather_plan(p):
    na = FIRST[p]
    nb = 64 - na
    ha, hb = (na // 2 + 7) // 8 * 8, (nb // 2 + 7) // 8 * 8
    own = [] if p == 0 else [(1, "XW")]
    msgs = []

    def add(name, step, owner, first, rows, deps):
        msgs.append(((p, *name), step, owner, first, rows, [d if d in own else (p, *d) for d in deps] if deps else own))

    for d in range(1, 5):
        for s in (1, -1):
            first, rows = (na, nb) if d < 4 else ((na, hb) if s > 0 else (na + hb, nb - hb))
            add(("BZ", s, d), (0, s), (0, -s * (d - 1)), first, rows, [("BZ", s, d - 1)] if d > 1 else [])
    add(("AY", 1, 1), (1, 0), (0, 0), 0, na, [])
    add(("AY", -1, 1), (-1, 0), (0, 0), 0, na, [])
    add(("AY", 1, 2), (1, 0), (-1, 0), 0, ha, [("AY", 1, 1)])
    add(("AY", -1, 2), (-1, 0), (1, 0), ha, na - ha, [("AY", -1, 1)])
    there = ([], [("AY", 1, 1)], [("AY", -1, 1)], [("AY", 1, 2), ("AY", -1, 2)])
    for d in range(1, 5):
        for j, oy in enumerate((0, -1, 1, 2)):
            for s in (1, -1):
                if d == 4 and (j < 2) != (s > 0):
                    continue
                deps = there[j] if d == 1 else [("AZ", s, d - 1, j)]
                add(("AZ", s, d, j), (0, s), (oy, -s * (d - 1)), 0, na, deps)
    for zz in (0, -1, 1, -2, 2, -3, 3, 4):
        deps = [] if zz == 0 else ([("BZ", 1, 4), ("BZ", -1, 4)] if zz == 4 else [("BZ", -1 if zz > 0 else 1, abs(zz))])
        for s in (1, -1):
            add(("BY", s, 1, zz), (s, 0), (0, zz), na, nb, deps)
        s = 1 if zz in (0, 1, -2, 3) else -1
        add(("BY", s, 2, zz), (s, 0), (-s, zz), na, nb, [("BY", s, 1, zz)])
    return msgs


def arrival_order(msgs):
    free, done, left = {}, set(), list(msgs)
    events, sends, waits = [(9.0, -1, (1, "XW"))], {}, []

    def issue(now):
        out = []
        for m in list(left):
            ahead = 1.5 if m[0][0] and any(o[0][0] == 0 and o[1] == m[1] for o in left) else 3.0
            if all(d in done for d in m[5]) and free.get(m[1], 0.0) - now < ahead:
                left.remove(m)
                begin = max(now, free.get(m[1], 0.0))
                free[m[1]] = begin + 1.4 * m[4] / 32
                heapq.heappush(events, (free[m[1]] + 2.2, len(msgs) - len(left), m[0]))
                out.append(m[0])
        return out

    sends[None] = issue(0.0)
    while events:
        now, _, name = heapq.heappop(events)
        done.add(name)
        waits.append(name)
        sends[name] = issue(now)
    assert not left
    return sends, waits


MSGS = gather_plan(0) + gather_plan(1)
INDEX = {m[0]: i for i, m in enumerate(MSGS)}
SENDS, WAITS = arrival_order(MSGS)
LAST0 = max(n for n, name in enumerate(WAITS) if name[0] == 0)


def kernel(
    chains, weights, vbias, hbias, temps, hthr, vthr, phase, accept,
    vis_out, hid_out, energy_out,
    W, V, CO, thr, TS, TR, hbr, L, acc, PA, H, HX, VX, SB, RB, meta, metar, swapv, swaph, vo, ho, BT, TU, TL, ebuf,
    gs, gr, dsem, xs, xr, ags, agr, rss, rsr, fs, fr, sws, swr, ms, mr, es, er, lsem,
):
    t = lax.axis_index("temp")
    m = lax.axis_index("mp")
    c = lax.rem(t, 2)
    z = lax.rem(t // 2, NZ)
    y = t // (2 * NZ)

    def col(d):
        return lax.rem(m + d + NX, NX)

    def rep(d):
        return lax.rem(t + d + NT, NT)

    def temp_of(dy, dz):
        return (lax.rem(y + dy + NY, NY) * NZ + lax.rem(z + dz + NZ, NZ)) * 2 + c

    step = 1 - 2 * lax.rem(m + c, 2)
    partner, other, far = (t, col(step)), (t, col(-step)), (t, col(2))
    a = lax.rem(m - c + NX, NX) // 2
    mine = pl.ds(pl.multiple_of(a * HALF, HALF), HALF)
    theirs = pl.ds(pl.multiple_of((1 - a) * HALF, HALF), HALF)

    def units(s, half, mate=False):
        if half:
            return col(step) if mate else m
        if s < SWEEPS - 1:
            return col(step + 2) if mate else col(2)
        return col(2) if mate else col(-step)

    pending = []

    def send(src, dst, ssem, rsem, device):
        copy = pltpu.make_async_remote_copy(
            src_ref=src, dst_ref=dst, send_sem=ssem, recv_sem=rsem, device_id=device, device_id_type=MESH
        )
        copy.start()
        return copy

    def arrived(ref, sem):
        pltpu.make_async_copy(ref, ref, sem).wait()

    def load(src, dst, i):
        copy = pltpu.make_async_copy(src, dst, lsem.at[i])
        copy.start()
        return copy

    block = pl.ds(pl.multiple_of(t * 64, 64), 64)
    wload = load(weights, W.at[0, block], 0)
    vload = [load(chains.at[mine, pl.ds(j * CW, CW)], V.at[0, 4 * m + j], 1 + j) for j in range(4)]
    oload = [load(chains.at[theirs, pl.ds(j * CW, CW)], CO.at[j], 5 + j) for j in range(4)]
    tload = {}
    for s in range(SWEEPS):
        tload[2 * s, 1] = load(hthr.at[s, theirs], thr.at[2 * s, 1], 9 + 4 * s)
        tload[2 * s, 0] = load(hthr.at[s, mine], thr.at[2 * s, 0], 10 + 4 * s)
        for p in range(2):
            cols = pl.ds(pl.multiple_of(units(s, 1 - p) * BLK, BLK), BLK)
            tload[2 * s + 1, p] = load(vthr.at[s, mine, cols], thr.at[2 * s + 1, p], 11 + 4 * s + p)
    beta = temps[0:1, 0:1]
    meta[...] = jnp.broadcast_to(beta, (8, 128))
    meta[0:2, :] = accept[...].astype(F32)

    barrier = pltpu.get_barrier_semaphore()
    peers = [(t, col(1)), (t, col(-1)), (t, col(2)), (rep(1), m), (rep(-1), m)]
    peers += [(temp_of(1, 0), m), (temp_of(-1, 0), m), (temp_of(0, 1), m), (temp_of(0, -1), m)]
    for peer in peers:
        pl.semaphore_signal(barrier, inc=1, device_id=peer, device_id_type=MESH)
    pl.semaphore_wait(barrier, len(peers))

    sibling = (t + 1 - 2 * c, m)

    def place(name, seen):
        p = name[0]
        _, (sy, sz), (oy, oz), first, rows, _ = MSGS[INDEX[name]]
        start = temp_of(oy - (sy if seen else 0), oz - (sz if seen else 0)) * 64 + first
        return W.at[p, pl.ds(pl.multiple_of(start, 8), rows)]

    def launch(name):
        i = INDEX[name]
        ref = place(name, False)
        pending.append(send(ref, ref, gs.at[i], gr.at[i], (temp_of(*MSGS[i][1]), m)))

    def to_sibling(p, ref):
        send(ref, ref, dsem.at[p, 0], dsem.at[p, 1], sibling)

    wload.wait()
    for name in SENDS[None]:
        launch(name)
    pending.append(send(W.at[0, block], W.at[1, block], xs.at[0], xr.at[0], far))
    to_sibling(0, W.at[0, block])
    for cp in vload:
        cp.wait()
    own_v = V.at[0, pl.ds(4 * m, 4)]
    pending.append(send(own_v, own_v, xs.at[1], xr.at[1], partner))
    for cp in oload:
        cp.wait()
    pending.append(send(CO, own_v, xs.at[2], xr.at[2], other))
    pending.append(send(CO, own_v, xs.at[3], xr.at[3], far))
    pending.append(send(hbias, hbr, xs.at[4], xr.at[4], far))
    for e in (0, 1):
        pending.append(send(meta, metar.at[e], ms.at[e], mr.at[e], (rep(1 - 2 * e), m)))

    def send_thresholds(s):
        tload[2 * s, 1].wait()
        TS[s] = thr[2 * s, 1].astype(F32).astype(BF16)
        pending.append(send(TS.at[s], TR.at[s], xs.at[5 + s], xr.at[5 + s], far))

    def prepare(k, p):
        if k % 2 == 0 and p == 1:
            arrived(TR.at[k // 2], xr.at[5 + k // 2])
            if k == 0:
                arrived(hbr, xr.at[4])
        else:
            tload[k, p].wait()

        def some(i, carry):
            r = pl.ds(pl.multiple_of(i * 32, 32), 32)
            if k % 2 == 0 and p == 1:
                value, bias = TR[k // 2, r, :], hbr[...]
            else:
                value, bias = thr[k, p, r, :], (hbias[...] if k % 2 == 0 else vbias[units(k // 2, 1 - p)])
            level = (value.astype(F32) + 0.5) / 256.0
            L[k, p, r, :] = beta * bias + (jnp.log(level) - jnp.log(1.0 - level))
            return carry

        lax.fori_loop(0, HALF // 32, some, 0)

    def decisions():
        for e in (0, 1):
            arrived(metar.at[e], mr.at[e])
        low, up = metar.at[0], metar.at[1]
        ph = phase[...]
        lower = (lax.rem(t, 2) == ph) & (t + 1 < NT)
        upper = (lax.rem(t + 1, 2) == ph) & (t >= 1)
        take_up = jnp.where(lower & (accept[...] == 1), 1.0, 0.0)
        take_low = jnp.where(upper & (low[0:2, :] > 0.5), 1.0, 0.0)
        b = jnp.where(take_up > 0.5, up[2:4, :], jnp.where(take_low > 0.5, low[2:4, :], jnp.broadcast_to(beta, (2, 128))))
        for h in (0, 1):
            for ref, rows in ((TU, take_up), (TL, take_low)):
                ref[128 * h : 128 * h + 128, :] = jnp.broadcast_to(rows[h : h + 1, :], (128, 128)).T
        BT[...] = jnp.broadcast_to(jnp.where(a == 0, b[0:1, :], b[1:2, :]), (128, 128)).T
        return take_up, take_low

    def dot(x, w):
        return jnp.dot(x, w, preferred_element_type=F32)

    def dot_t(x, w):
        return lax.dot_general(x, w, (((1,), (1,)), ((), ())), preferred_element_type=F32)

    def wrows(k):
        return pl.ds(pl.multiple_of(k * CW, CW), CW)

    def add_product(ph, p, chunks, fresh):
        for n in range(4):
            cols = pl.ds(n * CW, CW)
            total = None
            for k in chunks:
                part = dot(V[ph, k], W[p, wrows(k), cols])
                total = part if total is None else total + part
            acc[p, :, cols] = total if fresh else acc[p, :, cols] + total

    def hidden_states(s, p):
        def tile(n, carry):
            cols = pl.ds(pl.multiple_of(n * CW, CW), CW)
            H[s, p, :, cols] = jax.nn.sigmoid(beta * acc[p, :, cols] + L[2 * s, p, :, cols]).astype(BF16)
            return carry

        lax.fori_loop(0, 4, tile, 0)

    def first_half():
        half0 = W.at[0, pl.ds(0, NT // 2 * 64)]
        arrived(half0, dsem.at[0, 1])
        arrived(own_v, xr.at[1])
        arrived(own_v, xr.at[2])
        arrived(own_v, xr.at[3])
        add_product(0, 0, range(16), True)
        hidden_states(0, 0)

    def first_partials(g):
        def tile(j, carry):
            PA[4 * g + j] = dot_t(H[0, 0], W[0, wrows(4 * g + j), :])
            return carry

        lax.fori_loop(0, 4, tile, 0)

    flags = None
    early = [lambda: send_thresholds(0), lambda: send_thresholds(1)]
    early += [lambda k=k, p=p: prepare(k, p) for k, p in ((0, 0), (1, 0), (1, 1), (2, 0), (3, 0), (3, 1))]
    late = [first_half] + [lambda g=g: first_partials(g) for g in range(4)]
    late += [lambda: prepare(0, 1), lambda: prepare(2, 1)]
    for n, name in enumerate(WAITS):
        if name[1] == "XW":
            ref = W.at[1, block]
            arrived(ref, xr.at[0])
        else:
            ref = place(name, True)
            arrived(ref, gr.at[INDEX[name]])
        for nxt in SENDS[name]:
            launch(nxt)
        to_sibling(name[0], ref)
        if n >= 4 and n % 3 == 0 and early:
            early.pop(0)()
        if n == 32:
            flags = decisions()
        if n >= LAST0 + 2 and (n - LAST0) % 3 == 0 and late:
            late.pop(0)()
    for job in early + late:
        job()
    take_up, take_low = flags
    arrived(W.at[1, pl.ds(0, NT // 2 * 64)], dsem.at[1, 1])

    def partial(s, k):
        if s == 0:
            return PA[k] + dot_t(H[0, 1], W[1, wrows(k), :])
        return dot_t(H[s, 0], W[0, wrows(k), :]) + dot_t(H[s, 1], W[1, wrows(k), :])

    def visible_states(s):
        def give(h, carry):
            terms = []
            for i in (2 * h, 2 * h + 1):
                q = jnp.where(h < 2, units(s, 0, True), units(s, 1, True))
                terms.append(partial(s, 4 * q + lax.rem(i, 4)))
            for e in (0, 1):
                i = 2 * h + e
                SB[s, i] = terms[e].astype(BF16)
                send(SB.at[s, i], RB.at[s, i], rss.at[s, i], rsr.at[s, i], partner)
            return carry

        lax.fori_loop(0, 4, give, 0)

        def keep(half):
            def two(h, carry):
                own = [partial(s, 4 * units(s, half) + 2 * h + e) for e in (0, 1)]
                for e in (0, 1):
                    j = 2 * h + e
                    i = 4 * half + j
                    k = 4 * units(s, half) + j
                    arrived(RB.at[s, i], rsr.at[s, i])
                    cols = pl.ds(pl.multiple_of(j * CW, CW), CW)
                    pre = own[e] + RB[s, i].astype(F32)
                    V[s + 1, k] = jax.nn.sigmoid(beta * pre + L[2 * s + 1, 1 - half, :, cols]).astype(BF16)
                    ref = V.at[s + 1, k]
                    send(ref, ref, ags.at[s, i], agr.at[s, i], partner)
                    if s == SWEEPS - 1 and half == 0:
                        send(ref, VX.at[j], fs.at[1 + j], fr.at[1 + j], other)
                return carry

            lax.fori_loop(0, 2, two, 0)

        keep(0)
        keep(1)

    def gathered_product(ph):
        own = [4 * units(ph - 1, i // 4) + i % 4 for i in range(8)]
        for p in (0, 1):
            add_product(ph, p, own, True)
        for i in range(0, 8, 2):
            ks = [4 * units(ph - 1, i // 4, True) + i % 4 + e for e in (0, 1)]
            for e in (0, 1):
                arrived(V.at[ph, ks[e]], agr.at[ph - 1, i + e])
            for p in (0, 1):
                add_product(ph, p, ks, False)
            if ph == SWEEPS:
                swap_far(i // 2)

    def swap_far(j):
        arrived(VX.at[j], fr.at[1 + j])
        for e in (0, 1):
            ref = swapv.at[e, 1 - a, j]
            pending.append(send(VX.at[j], ref, sws.at[3 + j, e], swr.at[3 + j, e], (rep(1 - 2 * e), m)))

    add_product(0, 1, range(16), True)
    hidden_states(0, 1)
    visible_states(0)
    gathered_product(1)
    for p in (1, 0):
        hidden_states(1, p)
    pending.append(send(H.at[1, 1], HX, fs.at[0], fr.at[0], far))
    for e in (0, 1):
        pending.append(send(H.at[1, 0], swaph.at[e, a], sws.at[0, e], swr.at[0, e], (rep(1 - 2 * e), m)))
    visible_states(1)
    own_out = V.at[2, pl.ds(4 * m, 4)]
    for e in (0, 1):
        pending.append(send(own_out, swapv.at[e, a], sws.at[1, e], swr.at[1, e], (rep(1 - 2 * e), m)))
    arrived(HX, fr.at[0])
    for e in (0, 1):
        pending.append(send(HX, swaph.at[e, 1 - a], sws.at[2, e], swr.at[2, e], (rep(1 - 2 * e), m)))

    gathered_product(2)
    def lanes(g):
        return pl.ds(pl.multiple_of(g * 128, 128), 128)

    total = jnp.zeros((HALF, 128), F32)
    for p in (0, 1):
        q = units(SWEEPS - 1, 1 - p)

        def bias_part(g, value):
            return value + V[2, 4 * q + g // 2, :, lanes(lax.rem(g, 2))].astype(F32) * vbias[q, :, lanes(g)]

        total = lax.fori_loop(0, 8, bias_part, total)
    total = BT[...] * total
    for p in (0, 1):
        bias_ref = hbr if p else hbias

        def soft_part(g, value):
            x = BT[...] * (acc[p, :, lanes(g)] + bias_ref[:, lanes(g)])
            return value + (jnp.maximum(x, 0.0) + jnp.log1p(jnp.exp(-jnp.abs(x))))

        total = lax.fori_loop(0, 8, soft_part, total)
    ebuf[0, m] = jnp.broadcast_to(jnp.sum(total.T, axis=0, keepdims=True) * (-1.0 / NH), (8, 128))
    targets = [(0, d) for d in (1, 2, 3)] + [(e, d) for e in (1, -1) for d in range(4)]
    for e, d in targets:
        i = (e % 3) * 4 + d
        pending.append(send(ebuf.at[0, m], ebuf.at[e % 3, m], es.at[i], er.at[i], (rep(e), col(d))))

    for e in (0, 1):
        arrived(swaph.at[e, 0], swr.at[0, e])
        arrived(swaph.at[e, 1], swr.at[2, e])

    def chosen(rows, up, low, own):
        value = jnp.where(TL[rows, :] > 0.5, low.astype(F32), own.astype(F32))
        return jnp.where(TU[rows, :] > 0.5, up.astype(F32), value).astype(BF16)

    def swap_hidden(g, carry):
        cols = lanes(g)
        ho[mine, cols] = chosen(mine, swaph[1, a, :, cols], swaph[0, a, :, cols], H[1, 0, :, cols])
        ho[theirs, cols] = chosen(theirs, swaph[1, 1 - a, :, cols], swaph[0, 1 - a, :, cols], HX[:, cols])
        return carry

    lax.fori_loop(0, 8, swap_hidden, 0)
    hput = load(ho, hid_out, 17)
    for e in (0, 1):
        arrived(swapv.at[e, 0], swr.at[1, e])
        for j in range(4):
            arrived(swapv.at[e, 0, j], swr.at[3 + j, e])

    def swap_visible(g, carry):
        k, cols, out = g // 2, lanes(lax.rem(g, 2)), lanes(g)
        vo[mine, out] = chosen(mine, swapv[1, a, k, :, cols], swapv[0, a, k, :, cols], V[2, 4 * m + k, :, cols])
        vo[theirs, out] = chosen(theirs, swapv[1, 1 - a, k, :, cols], swapv[0, 1 - a, k, :, cols], VX[k, :, cols])
        return carry

    lax.fori_loop(0, 8, swap_visible, 0)
    vput = load(vo, vis_out, 18)
    for e, d in targets:
        arrived(ebuf.at[e % 3, col(-d)], er.at[(e % 3) * 4 + d])

    def summed(k):
        parity = c if k == 0 else 1 - c
        low = ebuf[k, parity, 0:1, :] + ebuf[k, parity + 1, 0:1, :]
        high = ebuf[k, parity + 2, 0:1, :] + ebuf[k, lax.rem(parity + 3, NX), 0:1, :]
        return low, high

    sums = [summed(k) for k in range(3)]
    for h in (0, 1):
        value = jnp.where(take_low[h : h + 1] > 0.5, sums[1][h], sums[0][h])
        energy_out[h : h + 1, :] = jnp.where(take_up[h : h + 1] > 0.5, sums[2][h], value)

    for copy in pending:
        copy.wait_send()
    for p in (0, 1):
        arrived(W.at[p, pl.ds(0, NT // 2 * 64)], dsem.at[p, 0])
    for s in range(SWEEPS):

        def left(i, carry):
            arrived(SB.at[s, i], rss.at[s, i])
            arrived(V.at[s + 1, i], ags.at[s, i])
            return carry

        lax.fori_loop(0, 8, left, 0)
    for j in range(4):
        arrived(VX.at[j], fs.at[1 + j])
    hput.wait()
    vput.wait()


def on_device(
    chains, weights, visible_bias, hidden_bias, inv_temps, hidden_thresholds, visible_thresholds, swap_phase, swap_accept
):
    vmem = pl.BlockSpec(memory_space=pltpu.VMEM)
    hbm = pl.BlockSpec(memory_space=pl.ANY)
    dma, mem = pltpu.SemaphoreType.DMA, pltpu.VMEM
    n = len(MSGS)
    vis, hid, energy = pl.pallas_call(
        kernel,
        out_shape=(
            jax.ShapeDtypeStruct((ROWS, BLK), BF16),
            jax.ShapeDtypeStruct((ROWS, BLK), BF16),
            jax.ShapeDtypeStruct((2, 128), F32),
        ),
        in_specs=[hbm, hbm, vmem, vmem, vmem, hbm, hbm, vmem, vmem],
        out_specs=(hbm, hbm, vmem),
        scratch_shapes=[
            mem((2, 4096, BLK), BF16),
            mem((3, 16, HALF, CW), BF16),
            mem((4, HALF, CW), BF16),
            mem((4, 2, HALF, BLK), I32),
            mem((2, HALF, BLK), BF16),
            mem((2, HALF, BLK), BF16),
            mem((1, BLK), F32),
            mem((4, 2, HALF, BLK), F32),
            mem((2, HALF, BLK), F32),
            mem((16, HALF, CW), F32),
            mem((2, 2, HALF, BLK), BF16),
            mem((HALF, BLK), BF16),
            mem((4, HALF, CW), BF16),
            mem((2, 8, HALF, CW), BF16),
            mem((2, 8, HALF, CW), BF16),
            mem((8, 128), F32),
            mem((2, 8, 128), F32),
            mem((2, 2, 4, HALF, CW), BF16),
            mem((2, 2, HALF, BLK), BF16),
            mem((ROWS, BLK), BF16),
            mem((ROWS, BLK), BF16),
            mem((HALF, 128), F32),
            mem((ROWS, 128), F32),
            mem((ROWS, 128), F32),
            mem((3, 4, 8, 128), F32),
            dma((n,)), dma((n,)), dma((2, 2)), dma((7,)), dma((7,)),
            dma((2, 8)), dma((2, 8)), dma((2, 8)), dma((2, 8)), dma((5,)), dma((5,)),
            dma((7, 2)), dma((7, 2)), dma((2,)), dma((2,)), dma((12,)), dma((12,)), dma((19,)),
        ],
        compiler_params=pltpu.CompilerParams(
            collective_id=0, has_side_effects=True, vmem_limit_bytes=58 * 2**20
        ),
        name="tempered",
    )(
        chains,
        weights,
        visible_bias.reshape(4, 1, BLK),
        hidden_bias.reshape(1, BLK),
        inv_temps.reshape(1, 1),
        hidden_thresholds,
        visible_thresholds,
        swap_phase.reshape(2, 128),
        swap_accept.reshape(2, 128),
    )
    return vis, hid, energy.reshape(ROWS)


def solution(mesh):
    return jax.shard_map(
        on_device,
        mesh=mesh,
        in_specs=(
            P("temp", "mp"),
            P("temp", "mp"),
            P(),
            P("mp"),
            P("temp"),
            P(None, "temp", "mp"),
            P(None, "temp", None),
            P(),
            P("temp"),
        ),
        out_specs=(P("temp", "mp"), P("temp", "mp"), P("temp")),
        check_vma=False,
    )
```

time: 283 us -> 118 us (0.42)
  waiting for transfers between devices: 121 us -> 0 us
  Pallas kernels: 0 us -> 110 us
  blocking collectives: 65.4 us -> 0 us
  starting transfers between devices: 29.6 us -> 0 us
  matrix products: 27.9 us -> 0 us
  between operations: 14.9 us -> 1.29 us
  local copies, waits for them, and re-layouts: 16.6 us -> 4.98 us
  other arithmetic: 6.24 us -> 0 us
    pallas_call x0 -> x1, Pallas kernels: none -> 110 us  [on_device(): pl.pallas_call(kernel, out_shape=(jax.ShapeDtypeStruct((ROWS, BLK), BF16)...]
    all_to_all x2 -> x0, blocking collectives: 55.9 us -> none  [the longest x1 28.8 us: copy_for_each(): return lax.all_to_all(copies, axis, split_axis=0, concat_axis=0, tiled=True)]
    all_to_all x3 -> x0, waiting for transfers between devices: 54.7 us -> none  [the longest x2 36.4 us: copy_for_each(): return lax.all_to_all(copies, axis, split_axis=0, concat_axis=0, tiled=True)]
    all_gather x1 -> x0, waiting for transfers between devices: 54 us -> none  [on_device(): weight_cols = lax.all_gather(weights, 'temp', axis=0, tiled=True)]
    dot_general x4 -> x0, matrix products: 27.9 us -> none  [the longest x2 15.1 us: on_device(): lax.dot_general(hidden, weight_cols, (((1,), (1,)), ((), ())), preferred_...]
    ppermute x5 -> x0, starting transfers between devices: 17.3 us -> none  [from_behind(): lax.ppermute(value, axis, [(source, source + steps) for source in range(f...]
    all_to_all x3 -> x0, starting transfers between devices: 12.3 us -> none  [the longest x2 8.03 us: copy_for_each(): return lax.all_to_all(copies, axis, split_axis=0, concat_axis=0, tiled=True)]
    ppermute x5 -> x0, waiting for transfers between devices: 11.7 us -> none  [from_behind(): lax.ppermute(value, axis, [(source, source + steps) for source in range(f...]
  transfers between devices with their start and end apart: 9 -> 0, of which waited for: 7 -> 0; matrix products, arithmetic and copies ran while one was open for 4% -> 0% of each run, Pallas kernels for 0% -> 0%
where the time goes in v3:
time: 118 us; the launch traced here: 116 us
  Pallas kernels  110 us (93%)
  local copies, waits for them, and re-layouts  4.98 us (4%)
  between operations  1.29 us (1%)
    pallas_call x1, Pallas kernels, on_device(): pl.pallas_call(kernel, out_shape=(jax.ShapeDtypeStruct((ROWS, BLK), BF16)...  110 us
    unnamed x3, local copies, waits for them, and re-layouts  4.98 us

profile of v3, /device:TPU:8, one launch (start us, length us, event | category | flops | bytes accessed | tf_op | source)
XLA Modules:
  0.0 116.5 jit_solution(16223708635948715584)
XLA Ops:
  1.3 110.2 %tempered.1 = (bf16[256,1024]{1,0:T(8,128)(2,1)}, bf16[256,1024]{1,0:T(8,128)(2,1)}, f32[2,128]{1,0:T(2,128)}) custom-call(bf16[256,1024]{1,0:T(8,128)(2,1)} %chains.1, bf16[64,1024]{1,0:T(8,128)(2,1)} %weights.1, f32[4,1,1024]{2,1,0:T(1,128)} %bitcast.7, f32[1,1024]{1,0:T(1,128)} %bitcast.8, f32[1,1]{1,0:T(1,128)} %bitcast.6.temps, s32[2,256,1024]{2,1,0:T(8,128)} %hthr.1, ...), custom_call_target="tpu_custom_call" | custom-call | tf_op jit(solution)/shard_map/tempered/pallas_call | solution.py:473
  111.5 1.9 %copy.16 = bf16[256,1024]{1,0:T(8,128)(2,1)} copy(bf16[256,1024]{1,0:T(8,128)(2,1)} %get-tuple-element.12) | data formatting | bytes 1048576
  113.4 1.9 %copy.17 = bf16[256,1024]{1,0:T(8,128)(2,1)} copy(bf16[256,1024]{1,0:T(8,128)(2,1)} %get-tuple-element.13) | data formatting | bytes 1048576
  115.3 1.2 %copy.18 = f32[256]{0:T(256)} copy(f32[256]{0:T(256)} %bitcast.11) | data formatting | bytes 2048

commit v4 on v3

--- a/solution.py
+++ b/solution.py
@@ -86,8 +86,8 @@
 def kernel(
     chains, weights, vbias, hbias, temps, hthr, vthr, phase, accept,
     vis_out, hid_out, energy_out,
-    W, V, CO, thr, TS, TR, hbr, L, acc, PA, H, HX, VX, SB, RB, meta, metar, swapv, swaph, vo, ho, BT, TU, TL, ebuf,
-    gs, gr, dsem, xs, xr, ags, agr, rss, rsr, fs, fr, sws, swr, ms, mr, es, er, lsem,
+    W, V, CO, thr, TS, TR, hbr, L, acc, PA, H, HX, VX, SB, RB, meta, metar, swapv, swaph, BT, TU, TL, ebuf,
+    gs, gr, dsem, xs, xr, ags, agr, rss, rsr, fs, fr, sws, swr, ms, es, lsem,
 ):
     t = lax.axis_index("temp")
     m = lax.axis_index("mp")
@@ -117,14 +117,11 @@
             return col(step + 2) if mate else col(2)
         return col(2) if mate else col(-step)
 
-    pending = []
-
     def send(src, dst, ssem, rsem, device):
         copy = pltpu.make_async_remote_copy(
             src_ref=src, dst_ref=dst, send_sem=ssem, recv_sem=rsem, device_id=device, device_id_type=MESH
         )
         copy.start()
-        return copy
 
     def arrived(ref, sem):
         pltpu.make_async_copy(ref, ref, sem).wait()
@@ -167,7 +164,7 @@
     def launch(name):
         i = INDEX[name]
         ref = place(name, False)
-        pending.append(send(ref, ref, gs.at[i], gr.at[i], (temp_of(*MSGS[i][1]), m)))
+        send(ref, ref, gs.at[name[0]], gr.at[i], (temp_of(*MSGS[i][1]), m))
 
     def to_sibling(p, ref):
         send(ref, ref, dsem.at[p, 0], dsem.at[p, 1], sibling)
@@ -175,30 +172,30 @@
     wload.wait()
     for name in SENDS[None]:
         launch(name)
-    pending.append(send(W.at[0, block], W.at[1, block], xs.at[0], xr.at[0], far))
+    send(W.at[0, block], W.at[1, block], xs.at[0], xr.at[0], far)
     to_sibling(0, W.at[0, block])
     for cp in vload:
         cp.wait()
     own_v = V.at[0, pl.ds(4 * m, 4)]
-    pending.append(send(own_v, own_v, xs.at[1], xr.at[1], partner))
+    send(own_v, own_v, xs.at[1], xr.at[1], partner)
     for cp in oload:
         cp.wait()
-    pending.append(send(CO, own_v, xs.at[2], xr.at[2], other))
-    pending.append(send(CO, own_v, xs.at[3], xr.at[3], far))
-    pending.append(send(hbias, hbr, xs.at[4], xr.at[4], far))
+    send(CO, own_v, xs.at[1], xr.at[1], other)
+    send(CO, own_v, xs.at[1], xr.at[1], far)
+    send(hbias, hbr, xs.at[2], xr.at[2], far)
     for e in (0, 1):
-        pending.append(send(meta, metar.at[e], ms.at[e], mr.at[e], (rep(1 - 2 * e), m)))
+        send(meta, metar.at[e], ms.at[0], ms.at[1], (rep(1 - 2 * e), m))
 
     def send_thresholds(s):
         tload[2 * s, 1].wait()
         TS[s] = thr[2 * s, 1].astype(F32).astype(BF16)
-        pending.append(send(TS.at[s], TR.at[s], xs.at[5 + s], xr.at[5 + s], far))
+        send(TS.at[s], TR.at[s], xs.at[3], xr.at[3 + s], far)
 
     def prepare(k, p):
         if k % 2 == 0 and p == 1:
-            arrived(TR.at[k // 2], xr.at[5 + k // 2])
+            arrived(TR.at[k // 2], xr.at[3 + k // 2])
             if k == 0:
-                arrived(hbr, xr.at[4])
+                arrived(hbr, xr.at[2])
         else:
             tload[k, p].wait()
 
@@ -215,8 +212,7 @@
         lax.fori_loop(0, HALF // 32, some, 0)
 
     def decisions():
-        for e in (0, 1):
-            arrived(metar.at[e], mr.at[e])
+        arrived(metar, ms.at[1])
         low, up = metar.at[0], metar.at[1]
         ph = phase[...]
         lower = (lax.rem(t, 2) == ph) & (t + 1 < NT)
@@ -259,9 +255,7 @@
     def first_half():
         half0 = W.at[0, pl.ds(0, NT // 2 * 64)]
         arrived(half0, dsem.at[0, 1])
-        arrived(own_v, xr.at[1])
-        arrived(own_v, xr.at[2])
-        arrived(own_v, xr.at[3])
+        arrived(V.at[0, pl.ds(0, 12)], xr.at[1])
         add_product(0, 0, range(16), True)
         hidden_states(0, 0)
 
@@ -304,59 +298,64 @@
         return dot_t(H[s, 0], W[0, wrows(k), :]) + dot_t(H[s, 1], W[1, wrows(k), :])
 
     def visible_states(s):
-        def give(h, carry):
-            terms = []
-            for i in (2 * h, 2 * h + 1):
-                q = jnp.where(h < 2, units(s, 0, True), units(s, 1, True))
-                terms.append(partial(s, 4 * q + lax.rem(i, 4)))
+        def give(i, term):
+            SB[s, i] = term.astype(BF16)
+            send(SB.at[s, i], RB.at[s, i], rss.at[s], rsr.at[s, i], partner)
+
+        def keep(i, own):
+            j, half = i % 4, i // 4
+            k = 4 * units(s, half) + j
+            arrived(RB.at[s, i], rsr.at[s, i])
+            pre = own + RB[s, i].astype(F32)
+            V[s + 1, k] = jax.nn.sigmoid(beta * pre + L[2 * s + 1, 1 - half, :, j * CW : j * CW + CW]).astype(BF16)
+            ref = V.at[s + 1, k]
+            send(ref, ref, ags.at[s], agr.at[s, i], partner)
+            if s < SWEEPS - 1:
+                return
+            if half == 0:
+                send(ref, VX.at[j], fs.at[1], fr.at[1 + j], other)
+                return
+            swap(ref, lambda e: swapv.at[e, a, j], 1)
+
+        jobs = [(give, i, 4 * units(s, i // 4, True) + i % 4) for i in range(8)]
+        jobs += [(keep, i, 4 * units(s, i // 4) + i % 4) for i in range(8)]
+        def terms(n):
+            return [partial(s, jobs[n + e][2]) for e in (0, 1)]
+
+        ahead = terms(0)
+        for n in range(0, len(jobs), 2):
+            now, ahead = ahead, (terms(n + 2) if n + 2 < len(jobs) else None)
             for e in (0, 1):
-                i = 2 * h + e
-                SB[s, i] = terms[e].astype(BF16)
-                send(SB.at[s, i], RB.at[s, i], rss.at[s, i], rsr.at[s, i], partner)
-            return carry
-
-        lax.fori_loop(0, 4, give, 0)
-
-        def keep(half):
-            def two(h, carry):
-                own = [partial(s, 4 * units(s, half) + 2 * h + e) for e in (0, 1)]
-                for e in (0, 1):
-                    j = 2 * h + e
-                    i = 4 * half + j
-                    k = 4 * units(s, half) + j
-                    arrived(RB.at[s, i], rsr.at[s, i])
-                    cols = pl.ds(pl.multiple_of(j * CW, CW), CW)
-                    pre = own[e] + RB[s, i].astype(F32)
-                    V[s + 1, k] = jax.nn.sigmoid(beta * pre + L[2 * s + 1, 1 - half, :, cols]).astype(BF16)
-                    ref = V.at[s + 1, k]
-                    send(ref, ref, ags.at[s, i], agr.at[s, i], partner)
-                    if s == SWEEPS - 1 and half == 0:
-                        send(ref, VX.at[j], fs.at[1 + j], fr.at[1 + j], other)
-                return carry
-
-            lax.fori_loop(0, 2, two, 0)
-
-        keep(0)
-        keep(1)
+                job, i, _ = jobs[n + e]
+                job(i, now[e])
+
+    def swap(src, dst, kind):
+        for e in (0, 1):
+
+            @pl.when(t + 1 < NT if e == 0 else t >= 1)
+            def _():
+                send(src, dst(e), sws.at[kind, e], swr.at[kind, e], (rep(1 - 2 * e), m))
 
     def gathered_product(ph):
         own = [4 * units(ph - 1, i // 4) + i % 4 for i in range(8)]
-        for p in (0, 1):
-            add_product(ph, p, own, True)
+        if ph == SWEEPS:
+            swap_far(0)
+        add_product(ph, 0, own, True)
+        if ph == SWEEPS:
+            swap_far(1)
+        add_product(ph, 1, own, True)
         for i in range(0, 8, 2):
             ks = [4 * units(ph - 1, i // 4, True) + i % 4 + e for e in (0, 1)]
             for e in (0, 1):
                 arrived(V.at[ph, ks[e]], agr.at[ph - 1, i + e])
             for p in (0, 1):
                 add_product(ph, p, ks, False)
-            if ph == SWEEPS:
-                swap_far(i // 2)
+            if ph == SWEEPS and i < 4:
+                swap_far(2 + i // 2)
 
     def swap_far(j):
         arrived(VX.at[j], fr.at[1 + j])
-        for e in (0, 1):
-            ref = swapv.at[e, 1 - a, j]
-            pending.append(send(VX.at[j], ref, sws.at[3 + j, e], swr.at[3 + j, e], (rep(1 - 2 * e), m)))
+        swap(VX.at[j], lambda e: swapv.at[e, 1 - a, j], 1)
 
     add_product(0, 1, range(16), True)
     hidden_states(0, 1)
@@ -364,16 +363,11 @@
     gathered_product(1)
     for p in (1, 0):
         hidden_states(1, p)
-    pending.append(send(H.at[1, 1], HX, fs.at[0], fr.at[0], far))
-    for e in (0, 1):
-        pending.append(send(H.at[1, 0], swaph.at[e, a], sws.at[0, e], swr.at[0, e], (rep(1 - 2 * e), m)))
+    send(H.at[1, 1], HX, fs.at[0], fr.at[0], far)
+    swap(H.at[1, 0], lambda e: swaph.at[e, a], 0)
     visible_states(1)
-    own_out = V.at[2, pl.ds(4 * m, 4)]
-    for e in (0, 1):
-        pending.append(send(own_out, swapv.at[e, a], sws.at[1, e], swr.at[1, e], (rep(1 - 2 * e), m)))
     arrived(HX, fr.at[0])
-    for e in (0, 1):
-        pending.append(send(HX, swaph.at[e, 1 - a], sws.at[2, e], swr.at[2, e], (rep(1 - 2 * e), m)))
+    swap(HX, lambda e: swaph.at[e, 1 - a], 0)
 
     gathered_product(2)
     def lanes(g):
@@ -396,15 +390,24 @@
             return value + (jnp.maximum(x, 0.0) + jnp.log1p(jnp.exp(-jnp.abs(x))))
 
         total = lax.fori_loop(0, 8, soft_part, total)
-    ebuf[0, m] = jnp.broadcast_to(jnp.sum(total.T, axis=0, keepdims=True) * (-1.0 / NH), (8, 128))
+    ebuf[m] = jnp.broadcast_to(jnp.sum(total.T, axis=0, keepdims=True) * (-1.0 / NH), (8, 128))
     targets = [(0, d) for d in (1, 2, 3)] + [(e, d) for e in (1, -1) for d in range(4)]
     for e, d in targets:
-        i = (e % 3) * 4 + d
-        pending.append(send(ebuf.at[0, m], ebuf.at[e % 3, m], es.at[i], er.at[i], (rep(e), col(d))))
-
-    for e in (0, 1):
-        arrived(swaph.at[e, 0], swr.at[0, e])
-        arrived(swaph.at[e, 1], swr.at[2, e])
+        send(ebuf.at[m], ebuf.at[(e % 3) * NX + m], es.at[0], es.at[1], (rep(e), col(d)))
+
+    def swapped(ref, kind):
+        for e in (0, 1):
+            there = t >= 1 if e == 0 else t + 1 < NT
+
+            @pl.when(there)
+            def _():
+                arrived(ref.at[e], swr.at[kind, e])
+
+            @pl.when(jnp.logical_not(there))
+            def _():
+                ref[e] = jnp.zeros(ref.shape[1:], BF16)
+
+    swapped(swaph, 0)
 
     def chosen(rows, up, low, own):
         value = jnp.where(TL[rows, :] > 0.5, low.astype(F32), own.astype(F32))
@@ -412,32 +415,26 @@
 
     def swap_hidden(g, carry):
         cols = lanes(g)
-        ho[mine, cols] = chosen(mine, swaph[1, a, :, cols], swaph[0, a, :, cols], H[1, 0, :, cols])
-        ho[theirs, cols] = chosen(theirs, swaph[1, 1 - a, :, cols], swaph[0, 1 - a, :, cols], HX[:, cols])
+        hid_out[mine, cols] = chosen(mine, swaph[1, a, :, cols], swaph[0, a, :, cols], H[1, 0, :, cols])
+        hid_out[theirs, cols] = chosen(theirs, swaph[1, 1 - a, :, cols], swaph[0, 1 - a, :, cols], HX[:, cols])
         return carry
 
     lax.fori_loop(0, 8, swap_hidden, 0)
-    hput = load(ho, hid_out, 17)
-    for e in (0, 1):
-        arrived(swapv.at[e, 0], swr.at[1, e])
-        for j in range(4):
-            arrived(swapv.at[e, 0, j], swr.at[3 + j, e])
+    swapped(swapv, 1)
 
     def swap_visible(g, carry):
         k, cols, out = g // 2, lanes(lax.rem(g, 2)), lanes(g)
-        vo[mine, out] = chosen(mine, swapv[1, a, k, :, cols], swapv[0, a, k, :, cols], V[2, 4 * m + k, :, cols])
-        vo[theirs, out] = chosen(theirs, swapv[1, 1 - a, k, :, cols], swapv[0, 1 - a, k, :, cols], VX[k, :, cols])
+        vis_out[mine, out] = chosen(mine, swapv[1, a, k, :, cols], swapv[0, a, k, :, cols], V[2, 4 * m + k, :, cols])
+        vis_out[theirs, out] = chosen(theirs, swapv[1, 1 - a, k, :, cols], swapv[0, 1 - a, k, :, cols], VX[k, :, cols])
         return carry
 
     lax.fori_loop(0, 8, swap_visible, 0)
-    vput = load(vo, vis_out, 18)
-    for e, d in targets:
-        arrived(ebuf.at[e % 3, col(-d)], er.at[(e % 3) * 4 + d])
+    arrived(ebuf.at[pl.ds(0, 11)], es.at[1])
 
     def summed(k):
         parity = c if k == 0 else 1 - c
-        low = ebuf[k, parity, 0:1, :] + ebuf[k, parity + 1, 0:1, :]
-        high = ebuf[k, parity + 2, 0:1, :] + ebuf[k, lax.rem(parity + 3, NX), 0:1, :]
+        low = ebuf[k * NX + parity, 0:1, :] + ebuf[k * NX + parity + 1, 0:1, :]
+        high = ebuf[k * NX + parity + 2, 0:1, :] + ebuf[k * NX + lax.rem(parity + 3, NX), 0:1, :]
         return low, high
 
     sums = [summed(k) for k in range(3)]
@@ -445,22 +442,26 @@
         value = jnp.where(take_low[h : h + 1] > 0.5, sums[1][h], sums[0][h])
         energy_out[h : h + 1, :] = jnp.where(take_up[h : h + 1] > 0.5, sums[2][h], value)
 
-    for copy in pending:
-        copy.wait_send()
     for p in (0, 1):
+        arrived(W.at[p, pl.ds(0, 31 * 64)], gs.at[p])
         arrived(W.at[p, pl.ds(0, NT // 2 * 64)], dsem.at[p, 0])
+    arrived(W.at[0, block], xs.at[0])
+    arrived(V.at[0, pl.ds(0, 12)], xs.at[1])
+    arrived(hbr, xs.at[2])
+    arrived(TR, xs.at[3])
+    arrived(metar, ms.at[0])
+    arrived(HX, fs.at[0])
+    arrived(VX, fs.at[1])
+    arrived(ebuf.at[pl.ds(0, 11)], es.at[0])
     for s in range(SWEEPS):
-
-        def left(i, carry):
-            arrived(SB.at[s, i], rss.at[s, i])
-            arrived(V.at[s + 1, i], ags.at[s, i])
-            return carry
-
-        lax.fori_loop(0, 8, left, 0)
-    for j in range(4):
-        arrived(VX.at[j], fs.at[1 + j])
-    hput.wait()
-    vput.wait()
+        arrived(SB.at[s], rss.at[s])
+        arrived(SB.at[s], ags.at[s])
+    for e in (0, 1):
+
+        @pl.when(t + 1 < NT if e == 0 else t >= 1)
+        def _():
+            arrived(swaph.at[e], sws.at[0, e])
+            arrived(swapv.at[e], sws.at[1, e])
 
 
 def on_device(
@@ -472,13 +473,9 @@
     n = len(MSGS)
     vis, hid, energy = pl.pallas_call(
         kernel,
-        out_shape=(
-            jax.ShapeDtypeStruct((ROWS, BLK), BF16),
-            jax.ShapeDtypeStruct((ROWS, BLK), BF16),
-            jax.ShapeDtypeStruct((2, 128), F32),
-        ),
+        out_shape=(mem((ROWS, BLK), BF16), mem((ROWS, BLK), BF16), mem((2, 128), F32)),
         in_specs=[hbm, hbm, vmem, vmem, vmem, hbm, hbm, vmem, vmem],
-        out_specs=(hbm, hbm, vmem),
+        out_specs=(vmem, vmem, vmem),
         scratch_shapes=[
             mem((2, 4096, BLK), BF16),
             mem((3, 16, HALF, CW), BF16),
@@ -499,15 +496,13 @@
             mem((2, 8, 128), F32),
             mem((2, 2, 4, HALF, CW), BF16),
             mem((2, 2, HALF, BLK), BF16),
-            mem((ROWS, BLK), BF16),
-            mem((ROWS, BLK), BF16),
             mem((HALF, 128), F32),
             mem((ROWS, 128), F32),
             mem((ROWS, 128), F32),
-            mem((3, 4, 8, 128), F32),
-            dma((n,)), dma((n,)), dma((2, 2)), dma((7,)), dma((7,)),
-            dma((2, 8)), dma((2, 8)), dma((2, 8)), dma((2, 8)), dma((5,)), dma((5,)),
-            dma((7, 2)), dma((7, 2)), dma((2,)), dma((2,)), dma((12,)), dma((12,)), dma((19,)),
+            mem((12, 8, 128), F32),
+            dma((2,)), dma((n,)), dma((2, 2)), dma((4,)), dma((5,)),
+            dma((2,)), dma((2, 8)), dma((2,)), dma((2, 8)), dma((2,)), dma((5,)),
+            dma((2, 2)), dma((2, 2)), dma((2,)), dma((2,)), dma((17,)),
         ],
         compiler_params=pltpu.CompilerParams(
             collective_id=0, has_side_effects=True, vmem_limit_bytes=58 * 2**20

time: 118 us -> 111 us (0.941)
  Pallas kernels: 110 us -> 106 us
  local copies, waits for them, and re-layouts: 4.98 us -> 2.15 us
    pallas_call x1, Pallas kernels: 110 us -> 106 us  [on_device(): pl.pallas_call(kernel, out_shape=(mem((ROWS, BLK), BF16), mem((ROWS, BLK)...]
    unnamed x3, local copies, waits for them, and re-layouts: 4.98 us -> 2.15 us
where the time goes in v4:
time: 111 us; the launch traced here: 110 us
  Pallas kernels  106 us (95%)
  local copies, waits for them, and re-layouts  2.15 us (2%)
  between operations  1.29 us (1%)
    pallas_call x1, Pallas kernels, on_device(): pl.pallas_call(kernel, out_shape=(mem((ROWS, BLK), BF16), mem((ROWS, BLK)...  106 us

profile of v4, /device:TPU:8, one launch (start us, length us, event | category | flops | bytes accessed | tf_op | source)
XLA Modules:
  0.0 109.8 jit_solution(7018249508192970004)
XLA Ops:
  1.3 106.4 %tempered.1 = (bf16[256,1024]{1,0:T(8,128)(2,1)S(1)}, bf16[256,1024]{1,0:T(8,128)(2,1)S(1)}, f32[2,128]{1,0:T(2,128)S(1)}) custom-call(bf16[256,1024]{1,0:T(8,128)(2,1)} %chains.1, bf16[64,1024]{1,0:T(8,128)(2,1)} %weights.1, f32[4,1,1024]{2,1,0:T(1,128)} %bitcast.8, f32[1,1024]{1,0:T(1,128)} %bitcast.9, f32[1,1]{1,0:T(1,128)} %bitcast.6.temps, ...), custom_call_target="tpu_custom_call" | custom-call | tf_op jit(solution)/shard_map/tempered/pallas_call | solution.py:474
  107.7 0.8 copy.15
  108.5 0.6 copy.17
  109.0 0.8 copy.16

commit v5 on v4

--- a/solution.py
+++ b/solution.py
@@ -13,7 +13,7 @@
 ROWS, HALF, BLK, CW = 256, 128, 1024, 256
 F32, BF16, I32 = jnp.float32, jnp.bfloat16, jnp.int32
 MESH = pl.DeviceIdType.MESH
-FIRST = (24, 24)
+FIRST = (24, 32)
 
 
 def gather_plan(p):
@@ -26,7 +26,8 @@
     def add(name, step, owner, first, rows, deps):
         msgs.append(((p, *name), step, owner, first, rows, [d if d in own else (p, *d) for d in deps] if deps else own))
 
-    for d in range(1, 5):
+    deepest = 4 - p
+    for d in range(1, deepest + 1):
         for s in (1, -1):
             first, rows = (na, nb) if d < 4 else ((na, hb) if s > 0 else (na + hb, nb - hb))
             add(("BZ", s, d), (0, s), (0, -s * (d - 1)), first, rows, [("BZ", s, d - 1)] if d > 1 else [])
@@ -35,35 +36,44 @@
     add(("AY", 1, 2), (1, 0), (-1, 0), 0, ha, [("AY", 1, 1)])
     add(("AY", -1, 2), (-1, 0), (1, 0), ha, na - ha, [("AY", -1, 1)])
     there = ([], [("AY", 1, 1)], [("AY", -1, 1)], [("AY", 1, 2), ("AY", -1, 2)])
-    for d in range(1, 5):
+    for d in range(1, deepest + 1):
         for j, oy in enumerate((0, -1, 1, 2)):
             for s in (1, -1):
                 if d == 4 and (j < 2) != (s > 0):
                     continue
                 deps = there[j] if d == 1 else [("AZ", s, d - 1, j)]
                 add(("AZ", s, d, j), (0, s), (oy, -s * (d - 1)), 0, na, deps)
-    for zz in (0, -1, 1, -2, 2, -3, 3, 4):
+    for zz in (0, -1, 1, -2, 2, -3, 3, 4)[: 8 - p]:
         deps = [] if zz == 0 else ([("BZ", 1, 4), ("BZ", -1, 4)] if zz == 4 else [("BZ", -1 if zz > 0 else 1, abs(zz))])
         for s in (1, -1):
             add(("BY", s, 1, zz), (s, 0), (0, zz), na, nb, deps)
         s = 1 if zz in (0, 1, -2, 3) else -1
         add(("BY", s, 2, zz), (s, 0), (-s, zz), na, nb, [("BY", s, 1, zz)])
+    if p == 1:
+        whole = {
+            0: [("AZ", 1, 4, 0), ("BZ", 1, 4), ("BZ", -1, 4)],
+            -1: [("AZ", 1, 4, 1), ("BY", 1, 1, 4)],
+            1: [("AZ", -1, 4, 2), ("BY", -1, 1, 4)],
+            2: [("AZ", -1, 4, 3), ("BY", -1, 2, 4)],
+        }
+        for oy, deps in whole.items():
+            msgs.append(((1, "XB", oy), None, (oy, 4), 0, 64, [(0, *d) for d in deps]))
     return msgs
 
 
 def arrival_order(msgs):
-    free, done, left = {}, set(), list(msgs)
+    free, done, left = {None: 29.5}, set(), list(msgs)
     events, sends, waits = [(9.0, -1, (1, "XW"))], {}, []
 
     def issue(now):
         out = []
         for m in list(left):
-            ahead = 1.5 if m[0][0] and any(o[0][0] == 0 and o[1] == m[1] for o in left) else 3.0
-            if all(d in done for d in m[5]) and free.get(m[1], 0.0) - now < ahead:
+            ahead = 3.0 if m[0][0] and any(o[0][0] == 0 and o[1] == m[1] for o in left) else 4.0
+            if all(d in done for d in m[5]) and (m[1] is None or free.get(m[1], 0.0) - now < ahead):
                 left.remove(m)
                 begin = max(now, free.get(m[1], 0.0))
                 free[m[1]] = begin + 1.4 * m[4] / 32
-                heapq.heappush(events, (free[m[1]] + 2.2, len(msgs) - len(left), m[0]))
+                heapq.heappush(events, (free[m[1]] + (2.2 if m[1] else 3.5), len(msgs) - len(left), m[0]))
                 out.append(m[0])
         return out
 
@@ -157,13 +167,18 @@
 
     def place(name, seen):
         p = name[0]
-        _, (sy, sz), (oy, oz), first, rows, _ = MSGS[INDEX[name]]
+        _, hop, (oy, oz), first, rows, _ = MSGS[INDEX[name]]
+        sy, sz = hop or (0, 0)
         start = temp_of(oy - (sy if seen else 0), oz - (sz if seen else 0)) * 64 + first
         return W.at[p, pl.ds(pl.multiple_of(start, 8), rows)]
 
     def launch(name):
         i = INDEX[name]
         ref = place(name, False)
+        if MSGS[i][1] is None:
+            start = pl.multiple_of(temp_of(*MSGS[i][2]) * 64, 64)
+            send(W.at[0, pl.ds(start, 64)], ref, gs.at[1], gr.at[i], far)
+            return
         send(ref, ref, gs.at[name[0]], gr.at[i], (temp_of(*MSGS[i][1]), m))
 
     def to_sibling(p, ref):
@@ -235,8 +250,8 @@
     def wrows(k):
         return pl.ds(pl.multiple_of(k * CW, CW), CW)
 
-    def add_product(ph, p, chunks, fresh):
-        for n in range(4):
+    def add_product(ph, p, chunks, fresh, tiles=range(4)):
+        for n in tiles:
             cols = pl.ds(n * CW, CW)
             total = None
             for k in chunks:
@@ -256,20 +271,16 @@
         half0 = W.at[0, pl.ds(0, NT // 2 * 64)]
         arrived(half0, dsem.at[0, 1])
         arrived(V.at[0, pl.ds(0, 12)], xr.at[1])
-        add_product(0, 0, range(16), True)
-        hidden_states(0, 0)
 
     def first_partials(g):
-        def tile(j, carry):
-            PA[4 * g + j] = dot_t(H[0, 0], W[0, wrows(4 * g + j), :])
-            return carry
-
-        lax.fori_loop(0, 4, tile, 0)
+        for k in (2 * g, 2 * g + 1):
+            PA[k] = dot_t(H[0, 0], W[0, wrows(k), :])
 
     flags = None
     early = [lambda: send_thresholds(0), lambda: send_thresholds(1)]
     early += [lambda k=k, p=p: prepare(k, p) for k, p in ((0, 0), (1, 0), (1, 1), (2, 0), (3, 0), (3, 1))]
-    late = [first_half] + [lambda g=g: first_partials(g) for g in range(4)]
+    late = [first_half] + [lambda n=n: add_product(0, 0, range(16), True, (n,)) for n in range(4)]
+    late += [lambda: hidden_states(0, 0)] + [lambda g=g: first_partials(g) for g in range(8)]
     late += [lambda: prepare(0, 1), lambda: prepare(2, 1)]
     for n, name in enumerate(WAITS):
         if name[1] == "XW":
@@ -285,7 +296,7 @@
             early.pop(0)()
         if n == 32:
             flags = decisions()
-        if n >= LAST0 + 2 and (n - LAST0) % 3 == 0 and late:
+        if n >= LAST0 + 4 and late:
             late.pop(0)()
     for job in early + late:
         job()
@@ -369,7 +380,6 @@
     arrived(HX, fr.at[0])
     swap(HX, lambda e: swaph.at[e, 1 - a], 0)
 
-    gathered_product(2)
     def lanes(g):
         return pl.ds(pl.multiple_of(g * 128, 128), 128)
 
@@ -382,12 +392,13 @@
 
         total = lax.fori_loop(0, 8, bias_part, total)
     total = BT[...] * total
+    gathered_product(2)
     for p in (0, 1):
         bias_ref = hbr if p else hbias
 
         def soft_part(g, value):
             x = BT[...] * (acc[p, :, lanes(g)] + bias_ref[:, lanes(g)])
-            return value + (jnp.maximum(x, 0.0) + jnp.log1p(jnp.exp(-jnp.abs(x))))
+            return value + (jnp.maximum(x, 0.0) + jnp.log(1.0 + jnp.exp(-jnp.abs(x))))
 
         total = lax.fori_loop(0, 8, soft_part, total)
     ebuf[m] = jnp.broadcast_to(jnp.sum(total.T, axis=0, keepdims=True) * (-1.0 / NH), (8, 128))

time: 111 us -> 108 us (0.973)
  Pallas kernels: 106 us -> 104 us
    pallas_call x1, Pallas kernels: 106 us -> 104 us  [on_device(): pl.pallas_call(kernel, out_shape=(mem((ROWS, BLK), BF16), mem((ROWS, BLK)...]
where the time goes in v5:
time: 108 us; the launch traced here: 107 us
  Pallas kernels  104 us (96%)
  local copies, waits for them, and re-layouts  2.15 us (2%)
  between operations  1.29 us (1%)
    pallas_call x1, Pallas kernels, on_device(): pl.pallas_call(kernel, out_shape=(mem((ROWS, BLK), BF16), mem((ROWS, BLK)...  104 us

profile of v5, /device:TPU:8, one launch (start us, length us, event | category | flops | bytes accessed | tf_op | source)
XLA Modules:
  0.0 107.4 jit_solution(11580829639557782201)
XLA Ops:
  1.3 104.0 %tempered.1 = (bf16[256,1024]{1,0:T(8,128)(2,1)S(1)}, bf16[256,1024]{1,0:T(8,128)(2,1)S(1)}, f32[2,128]{1,0:T(2,128)S(1)}) custom-call(bf16[256,1024]{1,0:T(8,128)(2,1)} %chains.1, bf16[64,1024]{1,0:T(8,128)(2,1)} %weights.1, f32[4,1,1024]{2,1,0:T(1,128)} %bitcast.8, f32[1,1024]{1,0:T(1,128)} %bitcast.9, f32[1,1]{1,0:T(1,128)} %bitcast.6.temps, ...), custom_call_target="tpu_custom_call" | custom-call | tf_op jit(solution)/shard_map/tempered/pallas_call | solution.py:485
  105.3 0.8 copy.15
  106.1 0.6 copy.17
  106.6 0.8 copy.16

commit v6 on v5

--- a/solution.py
+++ b/solution.py
@@ -13,6 +13,7 @@
 ROWS, HALF, BLK, CW = 256, 128, 1024, 256
 F32, BF16, I32 = jnp.float32, jnp.bfloat16, jnp.int32
 MESH = pl.DeviceIdType.MESH
+HY_AT = 12
 FIRST = (24, 32)
 
 
@@ -61,15 +62,21 @@
     return msgs
 
 
+def hop(name):
+    return (*name[:2], *name[3:]) if name[1] in ("AY", "AZ", "BZ", "BY") else name
+
+
 def arrival_order(msgs):
     free, done, left = {None: 29.5}, set(), list(msgs)
-    events, sends, waits = [(9.0, -1, (1, "XW"))], {}, []
+    events, sends, waits, due = [(9.0, -1, (1, "XW"))], {}, [], {}
+    for m in msgs:
+        due.setdefault(hop(m[0]), []).append(m[0])
 
     def issue(now):
         out = []
         for m in list(left):
             ahead = 3.0 if m[0][0] and any(o[0][0] == 0 and o[1] == m[1] for o in left) else 4.0
-            if all(d in done for d in m[5]) and (m[1] is None or free.get(m[1], 0.0) - now < ahead):
+            if all(d in ready for d in m[5]) and (m[1] is None or free.get(m[1], 0.0) - now < ahead):
                 left.remove(m)
                 begin = max(now, free.get(m[1], 0.0))
                 free[m[1]] = begin + 1.4 * m[4] / 32
@@ -77,26 +84,31 @@
                 out.append(m[0])
         return out
 
+    ready = set()
     sends[None] = issue(0.0)
     while events:
         now, _, name = heapq.heappop(events)
+        both = due.get(hop(name), [name])
         done.add(name)
-        waits.append(name)
-        sends[name] = issue(now)
+        if all(other in done for other in both):
+            ready.update(both)
+            waits.append(both)
+            sends[hop(name)] = issue(now)
     assert not left
     return sends, waits
 
 
 MSGS = gather_plan(0) + gather_plan(1)
 INDEX = {m[0]: i for i, m in enumerate(MSGS)}
+SEMS = {h: i for i, h in enumerate(dict.fromkeys(hop(m[0]) for m in MSGS))}
 SENDS, WAITS = arrival_order(MSGS)
-LAST0 = max(n for n, name in enumerate(WAITS) if name[0] == 0)
+LAST0 = max(n for n, names in enumerate(WAITS) if names[0][0] == 0)
 
 
 def kernel(
-    chains, weights, vbias, hbias, temps, hthr, vthr, phase, accept,
+    chains, weights, vbias_in, hbias_in, temps_in, hthr, vthr, phase_in, accept_in,
     vis_out, hid_out, energy_out,
-    W, V, CO, thr, TS, TR, hbr, L, acc, PA, H, HX, VX, SB, RB, meta, metar, swapv, swaph, BT, TU, TL, ebuf,
+    W, V, CO, thr, TS, TR, hbr, L, acc, PA, H, HX, VX, SB, RB, meta, metar, swapv, swaph, BT, TU, TL, ebuf, vbias, hbias, temps, phase, accept,
     gs, gr, dsem, xs, xr, ags, agr, rss, rsr, fs, fr, sws, swr, ms, es, lsem,
 ):
     t = lax.axis_index("temp")
@@ -152,9 +164,12 @@
         for p in range(2):
             cols = pl.ds(pl.multiple_of(units(s, 1 - p) * BLK, BLK), BLK)
             tload[2 * s + 1, p] = load(vthr.at[s, mine, cols], thr.at[2 * s + 1, p], 11 + 4 * s + p)
-    beta = temps[0:1, 0:1]
-    meta[...] = jnp.broadcast_to(beta, (8, 128))
-    meta[0:2, :] = accept[...].astype(F32)
+    small = [
+        pltpu.make_async_copy(src, dst, lsem.at[17 + i])
+        for i, (src, dst) in enumerate(((vbias_in, vbias), (hbias_in, hbias), (temps_in, temps), (phase_in, phase), (accept_in, accept)))
+    ]
+    for copy in small:
+        copy.start()
 
     barrier = pltpu.get_barrier_semaphore()
     peers = [(t, col(1)), (t, col(-1)), (t, col(2)), (rep(1), m), (rep(-1), m)]
@@ -163,6 +178,12 @@
         pl.semaphore_signal(barrier, inc=1, device_id=peer, device_id_type=MESH)
     pl.semaphore_wait(barrier, len(peers))
 
+    for copy in small:
+        copy.wait()
+    beta = temps[0]
+    meta[...] = jnp.full((8, 128), beta, F32)
+    meta[0:2, :] = accept[...].astype(F32)
+
     sibling = (t + 1 - 2 * c, m)
 
     def place(name, seen):
@@ -177,9 +198,9 @@
         ref = place(name, False)
         if MSGS[i][1] is None:
             start = pl.multiple_of(temp_of(*MSGS[i][2]) * 64, 64)
-            send(W.at[0, pl.ds(start, 64)], ref, gs.at[1], gr.at[i], far)
+            send(W.at[0, pl.ds(start, 64)], ref, gs.at[1], gr.at[SEMS[hop(name)]], far)
             return
-        send(ref, ref, gs.at[name[0]], gr.at[i], (temp_of(*MSGS[i][1]), m))
+        send(ref, ref, gs.at[name[0]], gr.at[SEMS[hop(name)]], (temp_of(*MSGS[i][1]), m))
 
     def to_sibling(p, ref):
         send(ref, ref, dsem.at[p, 0], dsem.at[p, 1], sibling)
@@ -234,7 +255,7 @@
         upper = (lax.rem(t + 1, 2) == ph) & (t >= 1)
         take_up = jnp.where(lower & (accept[...] == 1), 1.0, 0.0)
         take_low = jnp.where(upper & (low[0:2, :] > 0.5), 1.0, 0.0)
-        b = jnp.where(take_up > 0.5, up[2:4, :], jnp.where(take_low > 0.5, low[2:4, :], jnp.broadcast_to(beta, (2, 128))))
+        b = jnp.where(take_up > 0.5, up[2:4, :], jnp.where(take_low > 0.5, low[2:4, :], jnp.full((2, 128), beta, F32)))
         for h in (0, 1):
             for ref, rows in ((TU, take_up), (TL, take_low)):
                 ref[128 * h : 128 * h + 128, :] = jnp.broadcast_to(rows[h : h + 1, :], (128, 128)).T
@@ -282,22 +303,26 @@
     late = [first_half] + [lambda n=n: add_product(0, 0, range(16), True, (n,)) for n in range(4)]
     late += [lambda: hidden_states(0, 0)] + [lambda g=g: first_partials(g) for g in range(8)]
     late += [lambda: prepare(0, 1), lambda: prepare(2, 1)]
-    for n, name in enumerate(WAITS):
-        if name[1] == "XW":
-            ref = W.at[1, block]
-            arrived(ref, xr.at[0])
+    for n, names in enumerate(WAITS):
+        p = names[0][0]
+        if names[0][1] == "XW":
+            refs = [W.at[1, block]]
+            arrived(refs[0], xr.at[0])
         else:
-            ref = place(name, True)
-            arrived(ref, gr.at[INDEX[name]])
-        for nxt in SENDS[name]:
+            refs = [place(name, True) for name in names]
+            total = sum(MSGS[INDEX[name]][4] for name in names)
+            arrived(W.at[p, pl.ds(0, total)], gr.at[SEMS[hop(names[0])]])
+        for nxt in SENDS[hop(names[0])]:
             launch(nxt)
-        to_sibling(name[0], ref)
-        if n >= 4 and n % 3 == 0 and early:
+        for ref in refs:
+            to_sibling(p, ref)
+        if n >= 3 and n % 2 == 0 and early:
             early.pop(0)()
-        if n == 32:
+        if n == 18:
             flags = decisions()
-        if n >= LAST0 + 4 and late:
-            late.pop(0)()
+        for _ in range(2):
+            if n >= LAST0 + 2 and late:
+                late.pop(0)()
     for job in early + late:
         job()
     take_up, take_low = flags
@@ -339,6 +364,9 @@
             for e in (0, 1):
                 job, i, _ = jobs[n + e]
                 job(i, now[e])
+            if s == SWEEPS - 1 and n == HY_AT:
+                arrived(HX, fr.at[0])
+                swap(HX, lambda e: swaph.at[e, 1 - a], 0)
 
     def swap(src, dst, kind):
         for e in (0, 1):
@@ -377,8 +405,6 @@
     send(H.at[1, 1], HX, fs.at[0], fr.at[0], far)
     swap(H.at[1, 0], lambda e: swaph.at[e, a], 0)
     visible_states(1)
-    arrived(HX, fr.at[0])
-    swap(HX, lambda e: swaph.at[e, 1 - a], 0)
 
     def lanes(g):
         return pl.ds(pl.multiple_of(g * 128, 128), 128)
@@ -481,11 +507,11 @@
     vmem = pl.BlockSpec(memory_space=pltpu.VMEM)
     hbm = pl.BlockSpec(memory_space=pl.ANY)
     dma, mem = pltpu.SemaphoreType.DMA, pltpu.VMEM
-    n = len(MSGS)
+    n = len(SEMS)
     vis, hid, energy = pl.pallas_call(
         kernel,
         out_shape=(mem((ROWS, BLK), BF16), mem((ROWS, BLK), BF16), mem((2, 128), F32)),
-        in_specs=[hbm, hbm, vmem, vmem, vmem, hbm, hbm, vmem, vmem],
+        in_specs=[hbm] * 9,
         out_specs=(vmem, vmem, vmem),
         scratch_shapes=[
             mem((2, 4096, BLK), BF16),
@@ -511,9 +537,10 @@
             mem((ROWS, 128), F32),
             mem((ROWS, 128), F32),
             mem((12, 8, 128), F32),
+            mem((4, 1, BLK), F32), mem((1, BLK), F32), pltpu.SMEM((1,), F32), mem((2, 128), I32), mem((2, 128), I32),
             dma((2,)), dma((n,)), dma((2, 2)), dma((4,)), dma((5,)),
             dma((2,)), dma((2, 8)), dma((2,)), dma((2, 8)), dma((2,)), dma((5,)),
-            dma((2, 2)), dma((2, 2)), dma((2,)), dma((2,)), dma((17,)),
+            dma((2, 2)), dma((2, 2)), dma((2,)), dma((2,)), dma((22,)),
         ],
         compiler_params=pltpu.CompilerParams(
             collective_id=0, has_side_effects=True, vmem_limit_bytes=58 * 2**20
@@ -524,7 +551,7 @@
         weights,
         visible_bias.reshape(4, 1, BLK),
         hidden_bias.reshape(1, BLK),
-        inv_temps.reshape(1, 1),
+        inv_temps,
         hidden_thresholds,
         visible_thresholds,
         swap_phase.reshape(2, 128),

time: 108 us -> 106 us (0.981)
  Pallas kernels: 104 us -> 101 us
    pallas_call x1, Pallas kernels: 104 us -> 101 us  [on_device(): pl.pallas_call(kernel, out_shape=(mem((ROWS, BLK), BF16), mem((ROWS, BLK)...]
where the time goes in v6:
time: 106 us; the launch traced here: 105 us
  Pallas kernels  101 us (95%)
  local copies, waits for them, and re-layouts  2.15 us (2%)
  between operations  1.29 us (1%)
    pallas_call x1, Pallas kernels, on_device(): pl.pallas_call(kernel, out_shape=(mem((ROWS, BLK), BF16), mem((ROWS, BLK)...  101 us
    unnamed x3, local copies, waits for them, and re-layouts  2.15 us

profile of v6, /device:TPU:8, one launch (start us, length us, event | category | flops | bytes accessed | tf_op | source)
XLA Modules:
  0.0 104.8 jit_solution(17939193402180308058)
XLA Ops:
  1.3 101.4 %tempered.1 = (bf16[256,1024]{1,0:T(8,128)(2,1)S(1)}, bf16[256,1024]{1,0:T(8,128)(2,1)S(1)}, f32[2,128]{1,0:T(2,128)S(1)}) custom-call(bf16[256,1024]{1,0:T(8,128)(2,1)} %chains.1, bf16[64,1024]{1,0:T(8,128)(2,1)} %weights.1, f32[4,1,1024]{2,1,0:T(1,128)} %bitcast.6, f32[1,1024]{1,0:T(1,128)} %bitcast.7, f32[1]{0:T(128)S(6)} %copy.18.temps_in, ...), custom_call_target="tpu_custom_call" | custom-call | tf_op jit(solution)/shard_map/tempered/pallas_call | solution.py:511
  102.6 0.8 copy.15
  103.4 0.6 copy.17
  104.0 0.8 copy.16

commit v7 on v6

--- a/solution.py
+++ b/solution.py
@@ -13,6 +13,7 @@
 ROWS, HALF, BLK, CW = 256, 128, 1024, 256
 F32, BF16, I32 = jnp.float32, jnp.bfloat16, jnp.int32
 MESH = pl.DeviceIdType.MESH
+START = 4
 HY_AT = 12
 FIRST = (24, 32)
 
@@ -210,17 +211,19 @@
         launch(name)
     send(W.at[0, block], W.at[1, block], xs.at[0], xr.at[0], far)
     to_sibling(0, W.at[0, block])
-    for cp in vload:
-        cp.wait()
     own_v = V.at[0, pl.ds(4 * m, 4)]
-    send(own_v, own_v, xs.at[1], xr.at[1], partner)
-    for cp in oload:
-        cp.wait()
-    send(CO, own_v, xs.at[1], xr.at[1], other)
-    send(CO, own_v, xs.at[1], xr.at[1], far)
-    send(hbias, hbr, xs.at[2], xr.at[2], far)
     for e in (0, 1):
         send(meta, metar.at[e], ms.at[0], ms.at[1], (rep(1 - 2 * e), m))
+
+    def send_chains():
+        for cp in vload:
+            cp.wait()
+        send(own_v, own_v, xs.at[1], xr.at[1], partner)
+        for cp in oload:
+            cp.wait()
+        send(CO, own_v, xs.at[1], xr.at[1], other)
+        send(CO, own_v, xs.at[1], xr.at[1], far)
+        send(hbias, hbr, xs.at[2], xr.at[2], far)
 
     def send_thresholds(s):
         tload[2 * s, 1].wait()
@@ -298,11 +301,11 @@
             PA[k] = dot_t(H[0, 0], W[0, wrows(k), :])
 
     flags = None
-    early = [lambda: send_thresholds(0), lambda: send_thresholds(1)]
+    early = [send_chains, lambda: send_thresholds(0)]
     early += [lambda k=k, p=p: prepare(k, p) for k, p in ((0, 0), (1, 0), (1, 1), (2, 0), (3, 0), (3, 1))]
-    late = [first_half] + [lambda n=n: add_product(0, 0, range(16), True, (n,)) for n in range(4)]
+    late = [first_half, lambda: send_thresholds(1)] + [lambda n=n: add_product(0, 0, range(16), True, (n,)) for n in range(4)]
     late += [lambda: hidden_states(0, 0)] + [lambda g=g: first_partials(g) for g in range(8)]
-    late += [lambda: prepare(0, 1), lambda: prepare(2, 1)]
+    late += [lambda: prepare(0, 1)]
     for n, names in enumerate(WAITS):
         p = names[0][0]
         if names[0][1] == "XW":
@@ -316,7 +319,7 @@
             launch(nxt)
         for ref in refs:
             to_sibling(p, ref)
-        if n >= 3 and n % 2 == 0 and early:
+        if n >= START and n % 2 == 0 and early:
             early.pop(0)()
         if n == 18:
             flags = decisions()
@@ -383,6 +386,8 @@
         if ph == SWEEPS:
             swap_far(1)
         add_product(ph, 1, own, True)
+        if ph == 1:
+            prepare(2, 1)
         for i in range(0, 8, 2):
             ks = [4 * units(ph - 1, i // 4, True) + i % 4 + e for e in (0, 1)]
             for e in (0, 1):
@@ -400,9 +405,9 @@
     hidden_states(0, 1)
     visible_states(0)
     gathered_product(1)
-    for p in (1, 0):
-        hidden_states(1, p)
+    hidden_states(1, 1)
     send(H.at[1, 1], HX, fs.at[0], fr.at[0], far)
+    hidden_states(1, 0)
     swap(H.at[1, 0], lambda e: swaph.at[e, a], 0)
     visible_states(1)
 
@@ -499,6 +504,17 @@
         def _():
             arrived(swaph.at[e], sws.at[0, e])
             arrived(swapv.at[e], sws.at[1, e])
+
+
+def hand_out(vis, hid, energy, vis_out, hid_out, energy_out, sem):
+    copies = [
+        pltpu.make_async_copy(src, dst, sem.at[i])
+        for i, (src, dst) in enumerate(((vis, vis_out), (hid, hid_out), (energy, energy_out)))
+    ]
+    for copy in copies:
+        copy.start()
+    for copy in copies:
+        copy.wait()
 
 
 def on_device(
@@ -557,6 +573,18 @@
         swap_phase.reshape(2, 128),
         swap_accept.reshape(2, 128),
     )
+    vis, hid, energy = pl.pallas_call(
+        hand_out,
+        out_shape=(
+            jax.ShapeDtypeStruct((ROWS, BLK), BF16),
+            jax.ShapeDtypeStruct((ROWS, BLK), BF16),
+            jax.ShapeDtypeStruct((2, 128), F32),
+        ),
+        in_specs=[vmem, vmem, vmem],
+        out_specs=(hbm, hbm, hbm),
+        scratch_shapes=[dma((3,))],
+        name="hand_out",
+    )(*(pltpu.with_memory_space_constraint(x, pltpu.VMEM) for x in (vis, hid, energy)))
     return vis, hid, energy.reshape(ROWS)
 
 

time: 106 us -> 104 us (0.981)
  local copies, waits for them, and re-layouts: 2.15 us -> 0 us
    unnamed x3 -> x0, local copies, waits for them, and re-layouts: 2.15 us -> none
where the time goes in v7:
time: 104 us; the launch traced here: 103 us
  Pallas kernels  101 us (97%)
  between operations  1.45 us (1%)
    pallas_call x1, Pallas kernels, on_device(): pl.pallas_call(kernel, out_shape=(mem((ROWS, BLK), BF16), mem((ROWS, BLK)...  100 us

profile of v7, /device:TPU:8, one launch (start us, length us, event | category | flops | bytes accessed | tf_op | source)
XLA Modules:
  0.0 102.8 jit_solution(10218802504166575111)
XLA Ops:
  1.3 100.3 %tempered.1 = (bf16[256,1024]{1,0:T(8,128)(2,1)S(1)}, bf16[256,1024]{1,0:T(8,128)(2,1)S(1)}, f32[2,128]{1,0:T(2,128)S(1)}) custom-call(bf16[256,1024]{1,0:T(8,128)(2,1)} %chains.1, bf16[64,1024]{1,0:T(8,128)(2,1)} %weights.1, f32[4,1,1024]{2,1,0:T(1,128)} %bitcast.5, f32[1,1024]{1,0:T(1,128)} %bitcast.6, f32[1]{0:T(128)S(6)} %copy.12.temps_in, ...), custom_call_target="tpu_custom_call" | custom-call | tf_op jit(solution)/shard_map/tempered/pallas_call | solution.py:527
  101.6 1.0 hand_out.1
